TPU v7x, 32 devices: a whole 2x2x4 slice. The times are simulated.
32 devices in a mesh: gx: 4 (over x, core), gy: 4 (over z), gz: 2 (over y).
Axes of the slice: x: 2, y: 2, z: 4, core: 2. Of those that a mesh axis runs over, the one named last changes fastest.
Arguments:
- incidence: int32 [4, 4, 2, 2, 16, 8, 128], P('gx', 'gy', 'gz'), may hold values from 0 to 1, as said below
- live_counts: int32 [4, 4, 2, 2], P('gx', 'gy', 'gz'), may hold values from 1 to 16, as said below
- lame_first: float32 [4, 4, 2, 2, 16], P('gx', 'gy', 'gz'), may hold values from 0.5 to 2
- shear_modulus: float32 [4, 4, 2, 2, 16], P('gx', 'gy', 'gz'), may hold values from 0.5 to 4.5
- stretch: float32 [3, 4, 4, 2, 2, 16], P(None, 'gx', 'gy', 'gz'), may hold values from 0.5 to 2
Outputs:
- stiffness: float32 [4, 4, 2, 3, 128, 3, 128], P('gx', 'gy', 'gz')
Inputs may be any that keep to these rules, and one draw needn't show every extreme that they name: `incidence`: each element slot names 8 distinct nodes of the tile, some corners replaced by all-zero rows; corner 0 of every slot is always present. `live_counts`: among the 2 tiles of one element block and one node block, at least one has exactly 16 live slots.
All inputs are finite; a program needn't handle non-finite values.
Results may differ from a plain program's by a relative error of at most 0.000059.
Values sent between devices are 32-bit elements; how exact they have to be, the bound alone decides.
No kernel may reach another device: no remote copies, remote signals or barrier semaphores. Data moves between devices by JAX's collectives and lax.ppermute only.
A program may use at most 64 MiB of HBM per device.

v0:
```python
import math

import jax
import jax.numpy as jnp
import numpy as np
from jax import lax
from jax.sharding import PartitionSpec as P


def corner_table():
    corner_signs = np.array(
        [
            [sign_x, sign_y, sign_z]
            for sign_z in (-1.0, 1.0)
            for sign_y in (-1.0, 1.0)
            for sign_x in (-1.0, 1.0)
        ]
    )
    gauss_points = corner_signs / math.sqrt(3.0)
    shape_grads = np.zeros((8, 8, 3))
    for gauss_index in range(8):
        for corner_index in range(8):
            for axis_index in range(3):
                product_value = corner_signs[corner_index, axis_index] / 8.0
                for other_axis in range(3):
                    if other_axis != axis_index:
                        product_value = product_value * (
                            1.0
                            + corner_signs[corner_index, other_axis]
                            * gauss_points[gauss_index, other_axis]
                        )
                shape_grads[gauss_index, corner_index, axis_index] = product_value
    table_values = np.zeros((8, 3, 8, 3))
    for gauss_index in range(8):
        for first_corner in range(8):
            for first_axis in range(3):
                for second_corner in range(8):
                    for second_axis in range(3):
                        table_values[first_corner, first_axis, second_corner, second_axis] += (
                            shape_grads[gauss_index, first_corner, first_axis]
                            * shape_grads[gauss_index, second_corner, second_axis]
                        )
    return table_values


def element_matrices(first_param, shear_values, lengths):
    inverse = 2.0 / lengths
    scaling = inverse[:, None, :] * inverse[None, :, :]
    volume = lengths[0] * lengths[1] * lengths[2] / 8.0
    ref_table = jnp.asarray(corner_table(), jnp.float32)
    coupled = ref_table[None] * jnp.transpose(scaling, (2, 0, 1))[:, None, :, None, :]
    contracted = coupled[:, :, 0, :, 0] + coupled[:, :, 1, :, 1] + coupled[:, :, 2, :, 2]
    unit_matrix = jnp.eye(3, dtype=jnp.float32)
    matrices = first_param[:, None, None, None, None] * coupled + shear_values[
        :, None, None, None, None
    ] * (
        contracted[:, :, None, :, None] * unit_matrix[None, None, :, None, :]
        + jnp.transpose(coupled, (0, 1, 4, 3, 2))
    )
    return matrices * volume[:, None, None, None, None]


def assemble_block(matrices, onehot):
    spread = jnp.einsum("epiqj,eqb->epijb", matrices, onehot, precision=lax.Precision.HIGHEST)
    return jnp.einsum("epa,epijb->iajb", onehot, spread, precision=lax.Precision.HIGHEST)


def on_device(incidence, live_counts, lame_first, shear_modulus, stretch):
    local_tiles = incidence.shape[3]
    capacity = incidence.shape[4]
    tile_width = incidence.shape[6]
    onehot = incidence.reshape(local_tiles, capacity, 8, tile_width)
    alive_mask = jnp.arange(capacity, dtype=jnp.int32)[None, :] < live_counts.reshape(
        local_tiles, 1
    )
    first_param = lame_first.reshape(local_tiles, capacity)
    shear_values = shear_modulus.reshape(local_tiles, capacity)
    lengths = stretch.reshape(3, local_tiles, capacity)
    node_iota = lax.broadcasted_iota(jnp.int32, onehot.shape, 3)
    present = jnp.sum(onehot, axis=3) > 0
    position = jnp.sum(onehot * node_iota, axis=3)
    node_ids = jnp.where(present & alive_mask[:, :, None], position, -1)
    params = jnp.stack([first_param, shear_values, lengths[0], lengths[1], lengths[2]], axis=2)
    params = lax.all_to_all(params, "gz", split_axis=0, concat_axis=0, tiled=True)
    node_ids = lax.all_to_all(node_ids, "gz", split_axis=0, concat_axis=0, tiled=True)
    node_range = jnp.arange(tile_width, dtype=jnp.int32)

    def add_source(accumulated, packed):
        source_params, source_nodes = packed
        matrices = element_matrices(
            source_params[:, 0], source_params[:, 1], source_params[:, 2:].T
        )
        spread_onehot = (source_nodes[:, :, None] == node_range).astype(jnp.float32)
        return (accumulated + assemble_block(matrices, spread_onehot), None)

    initial = jnp.zeros((3, tile_width, 3, tile_width), jnp.float32)
    tile_block, unused = lax.scan(add_source, initial, (params, node_ids))
    tile_block = tile_block[None]
    diag_sum = jnp.trace(tile_block.reshape(3 * tile_width, 3 * tile_width))
    grand_total = lax.psum(diag_sum, ("gx", "gy", "gz"))
    tile_count = lax.axis_size("gx") * lax.axis_size("gy") * local_tiles
    mean_diag = grand_total / (3 * tile_width * tile_count)
    return (tile_block / mean_diag).reshape(1, 1, 1, 3, tile_width, 3, tile_width)


def solution(mesh):
    return jax.shard_map(
        on_device,
        mesh=mesh,
        in_specs=(
            P("gx", "gy", "gz", None, None, None, None),
            P("gx", "gy", "gz", None),
            P("gx", "gy", "gz", None, None),
            P("gx", "gy", "gz", None, None),
            P(None, "gx", "gy", "gz", None, None),
        ),
        out_specs=P("gx", "gy", "gz", None, None, None, None),
        check_vma=False,
    )
```

profile of v0, /device:TPU:0, one launch (start us, length us, event | category | flops | bytes accessed | tf_op | source)
XLA Modules:
  0.0 66.3 jit_solution(12074733732620666828)
XLA Ops:
  0.0 1.6 %fusion.13 = s32[2,16,8]{2,1,0:T(8,128)S(1)} fusion(s32[1,1,1,2,16,8,128]{6,5,4,3,2,1,0:T(8,128)} %param.8), kind=kLoop, calls=%fused_computation.28 | loop fusion | flops 65280 | bytes 132096 | tf_op jit(solution)/shard_map/reduce_sum | solution.py:81
  1.6 0.6 reduce_sum.28
  2.2 0.6 copy-done.6
  2.9 0.1 iota_compare_fusion.2
  3.0 0.1 and_select_fusion
  3.1 0.7 %reshape.102 = s32[2,1,128]{2,1,0:T(1,128)} reshape(s32[2,8,16]{2,1,0:T(8,128)S(1)} %bitcast.66) | data formatting | bytes 2048
  3.8 4.3 %all-to-all-start.1 = ((s32[2,1,128]{2,1,0:T(1,128)}), s32[2,1,128]{2,1,0:T(1,128)S(1)}, u32[]{:S(2)}, u32[]{:S(2)}) async-start(s32[2,1,128]{2,1,0:T(1,128)} %reshape.102), calls=%async_computation.1 | async-start | bytes 2048 | tf_op jit(solution)/shard_map/all_to_all | solution.py:85
  8.1 0.6 copy.22
  8.7 3.0 %all-to-all-done.1 = s32[2,1,128]{2,1,0:T(1,128)S(1)} async-done(((s32[2,1,128]{2,1,0:T(1,128)}), s32[2,1,128]{2,1,0:T(1,128)S(1)}, u32[]{:S(2)}, u32[]{:S(2)}) %all-to-all-start.1) | async-done | bytes 1056 | tf_op jit(solution)/shard_map/all_to_all | solution.py:85
  11.7 3.2 %all-to-all-start = ((f32[2,16,5]{1,2,0:T(8,128)}), f32[2,16,5]{1,2,0:T(8,128)S(1)}, u32[]{:S(2)}, u32[]{:S(2)}) async-start(f32[2,16,5]{1,2,0:T(8,128)} %copy.22), calls=%async_computation | async-start | bytes 16384 | tf_op jit(solution)/shard_map/all_to_all | solution.py:84
  14.9 0.5 broadcast.77
  15.4 0.6 reduce.2
  16.0 0.1 reshape.103
  16.1 2.6 %all-to-all-done = f32[2,16,5]{1,2,0:T(8,128)S(1)} async-done(((f32[2,16,5]{1,2,0:T(8,128)}), f32[2,16,5]{1,2,0:T(8,128)S(1)}, u32[]{:S(2)}, u32[]{:S(2)}) %all-to-all-start) | async-done | bytes 672 | tf_op jit(solution)/shard_map/all_to_all | solution.py:84
  18.7 4.9 %while.12 = (s32[]{:T(128)}, f32[3,128,3,128]{1,3,0,2:T(8,128)S(1)}, f32[2,16,5]{1,2,0:T(8,128)S(1)}, s32[2,16,8]{1,2,0:T(8,128)S(1)}, s32[]{:T(128)}, /*index=5...) while((s32[]{:T(128)}, f32[3,128,3,128]{1,3,0,2:T(8,128)S(1)}, ...), condition=%wide.region_3.4_spmd.clone.clone, body=%wide.region_2.3_spmd.sunk.clone.clone.sunk | while | flops 241061120 | bytes 3757743 | solution.py:97
  18.7 0.1 broadcast_multiply_fusion.5
  18.9 0.2 add_multiply_fusion.2
  19.2 0.3 copy.41
  19.5 0.1 copy.42
  19.5 0.7 %fusion.29 = f32[16,8,3,3,128]{4,1,2,3,0:T(8,128)S(1)} fusion(f32[16,8,3,8,3]{3,1,2,4,0:T(8,128)S(1)} %copy.41, s32[16,8]{1,0:T(8,128)S(1)} %copy.42), kind=kOutput, calls=%fused_computation.9.clone.1 | convolution fusion | flops 14172160 | bytes 627200 | tf_op jit(solution)/shard_map/while/body/eval_jaxpr/epiqj,eqb->epijb/dot_general | solution.py:64
  20.2 0.7 %fusion.30 = f32[3,3,128,128,1]{3,2,1,0,4:T(8,128)S(1)} fusion(f32[16,8,3,3,128]{4,1,2,3,0:T(8,128)S(1)} %fusion.29, s32[16,8]{1,0:T(8,128)S(1)} %copy.42), kind=kOutput, calls=%fused_computation.2.clone.1 | convolution fusion | flops 226508800 | bytes 1180160 | tf_op jit(solution)/shard_map/while/body/eval_jaxpr/epa,epijb->iajb/dot_general | solution.py:65
  20.9 0.2 bitcast_add_fusion.2
  21.2 0.1 broadcast_multiply_fusion.5
  21.4 0.2 add_multiply_fusion.2
  21.6 0.3 copy.41
  22.0 0.7 %fusion.29 = f32[16,8,3,3,128]{4,1,2,3,0:T(8,128)S(1)} fusion(f32[16,8,3,8,3]{3,1,2,4,0:T(8,128)S(1)} %copy.41, s32[16,8]{1,0:T(8,128)S(1)} %copy.42), kind=kOutput, calls=%fused_computation.9.clone.1 | convolution fusion | flops 14172160 | bytes 627200 | tf_op jit(solution)/shard_map/while/body/eval_jaxpr/epiqj,eqb->epijb/dot_general | solution.py:64
  22.7 0.7 %fusion.30 = f32[3,3,128,128,1]{3,2,1,0,4:T(8,128)S(1)} fusion(f32[16,8,3,3,128]{4,1,2,3,0:T(8,128)S(1)} %fusion.29, s32[16,8]{1,0:T(8,128)S(1)} %copy.42), kind=kOutput, calls=%fused_computation.2.clone.1 | convolution fusion | flops 226508800 | bytes 1180160 | tf_op jit(solution)/shard_map/while/body/eval_jaxpr/epa,epijb->iajb/dot_general | solution.py:65
  23.4 0.2 bitcast_add_fusion.2
  23.6 0.8 %select_reduce_fusion = f32[]{:T(128)} fusion(f32[3,128,3,128]{1,3,0,2:T(8,128)S(1)} %get-tuple-element.37, s32[3,128]{1,0:T(4,128)S(1)} %multiply_add_fusion), kind=kLoop, calls=%fused_computation.26 | loop fusion | flops 442367 | bytes 591364 | tf_op jit(solution)/shard_map/jit(trace)/reduce_sum | solution.py:99
  24.4 0.2 copy.24
  24.6 40.2 %psum.7 = f32[]{:T(128)} all-reduce(f32[]{:T(128)} %select_reduce_fusion), channel_id=1, replica_groups=mesh['gx'=4,'gy'=4,'gz'=2] {'gx','gy','gz'}, use_global_device_ids=true, to_apply=%region_5.6 | all-reduce | flops 1 | bytes 8 | tf_op jit(solution)/shard_map/psum | solution.py:100
  65.4 0.9 %divide_bitcast_fusion = f32[1,1,1,3,128,3,128]{6,4,5,3,2,1,0:T(8,128)} fusion(f32[3,128,3,128]{3,1,2,0:T(8,128)S(1)} %copy.24, f32[]{:T(128)S(6)} %div.19), kind=kLoop, calls=%fused_computation.25 | loop fusion | flops 147456 | bytes 1179652 | tf_op jit(solution)/shard_map/reshape | solution.py:103
  (38 shorter events, 0.3 us)
Async XLA Ops:
  0.0 1.6 %copy-start.2 = (s32[1,1,1,2,16,8,128]{6,5,4,3,2,1,0:T(8,128)S(1)}, s32[1,1,1,2,16,8,128]{6,5,4,3,2,1,0:T(8,128)}, u32[]{:S(2)}) copy-start(s32[1,1,1,2,16,8,128]{6,5,4,3,2,1,0:T(8,128)} %param.8) | copy-start | bytes 393220
  2.2 0.7 copy-start.6
  2.9 5.1 %copy-start.4 = (f32[1,1,1,2,16]{4,3,2,1,0:T(2,128)S(1)}, f32[1,1,1,2,16]{4,3,2,1,0:T(2,128)}, u32[]{:S(2)}) copy-start(f32[1,1,1,2,16]{4,3,2,1,0:T(2,128)} %param.10) | copy-start | bytes 388
  3.0 5.1 %copy-start.5 = (f32[1,1,1,2,16]{4,3,2,1,0:T(2,128)S(1)}, f32[1,1,1,2,16]{4,3,2,1,0:T(2,128)}, u32[]{:S(2)}) copy-start(f32[1,1,1,2,16]{4,3,2,1,0:T(2,128)} %param.11) | copy-start | bytes 388
  3.0 5.1 %copy-start.3 = (f32[3,1,1,1,2,16]{5,4,3,2,1,0:T(2,128)S(1)}, f32[3,1,1,1,2,16]{5,4,3,2,1,0:T(2,128)}, u32[]{:S(2)}) copy-start(f32[3,1,1,1,2,16]{5,4,3,2,1,0:T(2,128)} %param.12) | copy-start | bytes 1156
  3.0 15.7 %copy-start = (f32[8,3,8,3]{2,3,1,0:T(4,128)S(1)}, f32[8,3,8,3]{2,3,1,0:T(4,128)}, u32[]{:S(2)}) copy-start(f32[8,3,8,3]{2,3,1,0:T(4,128)} %constant.33.clone..sunk.3) | copy-start | bytes 6916
  3.0 15.7 %copy-start.1 = (f32[8,3,8,3]{2,3,1,0:T(4,128)S(1)}, f32[8,3,8,3]{2,3,1,0:T(4,128)}, u32[]{:S(2)}) copy-start(f32[8,3,8,3]{2,3,1,0:T(4,128)} %constant.65) | copy-start | bytes 6916
  3.8 7.9 %all-to-all-start.1 = ((s32[2,1,128]{2,1,0:T(1,128)}), s32[2,1,128]{2,1,0:T(1,128)S(1)}, u32[]{:S(2)}, u32[]{:S(2)}) async-start(s32[2,1,128]{2,1,0:T(1,128)} %reshape.102), calls=%async_computation.1 | async-start | bytes 2048 | tf_op jit(solution)/shard_map/all_to_all | solution.py:85
  11.7 7.0 %all-to-all-start = ((f32[2,16,5]{1,2,0:T(8,128)}), f32[2,16,5]{1,2,0:T(8,128)S(1)}, u32[]{:S(2)}, u32[]{:S(2)}) async-start(f32[2,16,5]{1,2,0:T(8,128)} %copy.22), calls=%async_computation | async-start | bytes 16384 | tf_op jit(solution)/shard_map/all_to_all | solution.py:84
where the time goes:
time: 66.8 us; the launch traced here: 66.3 us
  blocking collectives  40.2 us (60%)
  starting transfers between devices  7.49 us (11%)
  other arithmetic  5.81 us (9%)
  waiting for transfers between devices  5.58 us (8%)
  local copies, waits for them, and re-layouts  3.6 us (5%)
  matrix products  2.72 us (4%)
  between operations  0.74 us (1%)
    psum x1, blocking collectives, on_device(): grand_total = lax.psum(diag_sum, ('gx', 'gy', 'gz'))  40.2 us
    all_to_all x1, starting transfers between devices, on_device(): lax.all_to_all(node_ids, 'gz', split_axis=0, concat_axis=0, tiled=True)  4.26 us
    all_to_all x1, starting transfers between devices, on_device(): lax.all_to_all(params, 'gz', split_axis=0, concat_axis=0, tiled=True)  3.23 us
    all_to_all x1, waiting for transfers between devices, on_device(): lax.all_to_all(node_ids, 'gz', split_axis=0, concat_axis=0, tiled=True)  2.96 us
    all_to_all x1, waiting for transfers between devices, on_device(): lax.all_to_all(params, 'gz', split_axis=0, concat_axis=0, tiled=True)  2.61 us
    reduce_sum x1, other arithmetic, on_device(): position = jnp.sum(onehot * node_iota, axis=3)  1.59 us
    unnamed x20, local copies, waits for them, and re-layouts  1.46 us
    dot_general x2, matrix products, assemble_block(): jnp.einsum('epa,epijb->iajb', onehot, spread, precision=lax.Precision.HIG...  1.37 us
  transfers between devices with their start and end apart: 2, of which 2 were waited for; matrix products, arithmetic and copies ran while one was open for 3% of the time, Pallas kernels for 0%

commit v1 on v0

v1 whole, which is shorter than its diff:
```python
import functools
import math

import jax
import jax.numpy as jnp
from jax import lax
from jax.experimental import pallas as pl
from jax.experimental.pallas import tpu as pltpu
from jax.sharding import PartitionSpec as P

AXES = ("gx", "gy", "gz")
CORNERS = 8
VMEM_LIMIT = 16 * 2**20
ROWS = 8
DIAGONAL = 2.0 / 9.0


def last_contraction(left, right):
    return lax.dot_general(
        left, right, (((1,), (1,)), ((), ())), preferred_element_type=jnp.float32
    )


def spread_lanes(values, cap):
    width = values.shape[1]
    step = cap
    while step < width:
        values = values + pltpu.roll(values, step, axis=1)
        step *= 2
    return values


def encode_kernel(inc_ref, live_ref, lame_ref, shear_ref, stretch_ref, parts_ref, pay_ref):
    tiles, cap, corners, width = inc_ref.shape
    lanes = corners * cap
    row = lax.broadcasted_iota(jnp.int32, (ROWS, width), 0)
    node = lax.broadcasted_iota(jnp.int32, (ROWS, width), 1)
    reader = jnp.where(row == 0, node, (row == 1).astype(jnp.int32))
    reader = reader.astype(jnp.float32).astype(jnp.bfloat16)
    slot = lax.broadcasted_iota(jnp.int32, (1, lanes), 1) % cap
    partial = jnp.zeros((1, lanes), jnp.float32)
    for t in range(tiles):
        onehot = jnp.concatenate([inc_ref[t, :, p, :] for p in range(corners)], axis=0)
        onehot = onehot.astype(jnp.float32).astype(jnp.bfloat16)
        found = last_contraction(reader, onehot)
        here = (found[1:2] > 0.5) & (slot < live_ref[0, t])
        pay_ref[t] = jnp.zeros((ROWS, lanes), jnp.float32)
        pay_ref[t, 1:2, :cap] = lame_ref[t : t + 1]
        pay_ref[t, 2:3, :cap] = shear_ref[t : t + 1]
        for k in range(3):
            pay_ref[t, 3 + k : 4 + k, :cap] = stretch_ref[k, t : t + 1]
        spread = spread_lanes(pay_ref[t], cap)
        lame, shear = spread[1:2], spread[2:3]
        h0, h1, h2 = spread[3:4], spread[4:5], spread[5:6]
        inverse0, inverse1, inverse2 = 2.0 / h0, 2.0 / h1, 2.0 / h2
        squares = inverse0 * inverse0 + inverse1 * inverse1 + inverse2 * inverse2
        volume = h0 * h1 * h2 / 8.0
        weight = volume * (lame + 4.0 * shear) * squares * DIAGONAL
        partial = partial + jnp.where(here, weight, 0.0)
        pay_ref[t] = spread
        pay_ref[t, 0:1] = jnp.where(here, found[0:1], -1.0)
    parts_ref[...] = jnp.broadcast_to(partial, parts_ref.shape)


def walsh(cap, lanes, mask):
    line = lax.broadcasted_iota(jnp.int32, (lanes, lanes), 0)
    column = lax.broadcasted_iota(jnp.int32, (lanes, lanes), 1)
    odd = (column // cap ^ mask) & ~(line // cap)
    odd = (odd ^ odd >> 1 ^ odd >> 2) & 1
    signs = jnp.where(line % cap == column % cap, 1 - 2 * odd, 0)
    return signs.astype(jnp.float32).astype(jnp.bfloat16)


def assemble(sources, cap, width, block_ref):
    lanes = sources[0].shape[1]
    masks = {(0, 1): 3, (0, 2): 5, (1, 2): 6}
    tables = {mask: walsh(cap, lanes, mask) for mask in (0, 3, 5, 6)}
    mode = lax.broadcasted_iota(jnp.int32, (1, lanes), 1) // cap
    bits = [mode >> k & 1 for k in range(3)]
    thirds = [jnp.where(bit == 1, 1.0 / 3.0, 1.0) for bit in bits]
    node = lax.broadcasted_iota(jnp.int32, (width, lanes), 0).astype(jnp.float32)
    high, low, right = {}, {}, {mask: [] for mask in tables}
    for source in sources:
        onehot = (node == source[0:1]).astype(jnp.float32).astype(jnp.bfloat16)
        modes = {
            mask: jnp.dot(onehot, table, preferred_element_type=jnp.float32)
            for mask, table in tables.items()
        }
        for mask in tables:
            right[mask].append(modes[mask].astype(jnp.bfloat16))
        lame, shear = source[1:2], source[2:3]
        lengths = [source[3 + k : 4 + k] for k in range(3)]
        inverse = [2.0 / length for length in lengths]
        scale = lengths[0] * lengths[1] * lengths[2] / 64.0
        squares = []
        for k in range(3):
            others = thirds[(k + 1) % 3] * thirds[(k + 2) % 3]
            squares.append(jnp.where(bits[k] == 1, others, 0.0) * inverse[k] * inverse[k])
        trace = shear * (squares[0] + squares[1] + squares[2])
        for i in range(3):
            for j in range(3):
                if i == j:
                    factor = scale * ((lame + shear) * squares[i] + trace)
                else:
                    material = jnp.where(bits[i] == 1, lame, shear)
                    factor = scale * inverse[i] * inverse[j] * thirds[3 - i - j] * material
                    factor = jnp.where(bits[i] != bits[j], factor, 0.0)
                weighted = modes[0] * factor
                top = weighted.astype(jnp.bfloat16)
                rest = (weighted - top.astype(jnp.float32)).astype(jnp.bfloat16)
                high.setdefault((i, j), []).append(top)
                low.setdefault((i, j), []).append(rest)
    for mask in right:
        right[mask] = jnp.concatenate(right[mask], axis=1)
    for i in range(3):
        for j in range(3):
            other = right[masks[min(i, j), max(i, j)] if i != j else 0]
            block_ref[i, j] = last_contraction(
                jnp.concatenate(high[i, j], axis=1), other
            ) + last_contraction(jnp.concatenate(low[i, j], axis=1), other)


def pair_kernel(cap, own_ref, other_ref, block_ref):
    me = lax.axis_index("gz")
    assemble([own_ref[me], other_ref[me]], cap, block_ref.shape[2], block_ref)


def many_kernel(cap, all_ref, block_ref):
    sources = [all_ref[z] for z in range(all_ref.shape[0])]
    assemble(sources, cap, block_ref.shape[2], block_ref)


def scale_kernel(entries, parts_ref, block_ref, out_ref, scaled, done):
    mean = jnp.sum(parts_ref[...]) / entries
    copies = []
    for i in range(3):
        for j in range(3):
            scaled[i, j] = block_ref[i, j] / mean
            copy = pltpu.make_async_copy(scaled.at[i, j], out_ref.at[i, j], done.at[i, j])
            copy.start()
            copies.append(copy)
    for copy in copies:
        copy.wait()


def on_device(incidence, live_counts, lame_first, shear_modulus, stretch):
    tiles, cap, corners, width = incidence.shape[3:]
    lanes = corners * cap
    devices = math.prod(lax.axis_size(a) for a in AXES)
    depth = lax.axis_size("gz")
    vmem = pl.BlockSpec(memory_space=pltpu.VMEM)
    smem = pl.BlockSpec(memory_space=pltpu.SMEM)
    anywhere = pl.BlockSpec(memory_space=pl.ANY)
    parts, payload = pl.pallas_call(
        encode_kernel,
        out_shape=(
            jax.ShapeDtypeStruct((devices, lanes), jnp.float32),
            jax.ShapeDtypeStruct((tiles, ROWS, lanes), jnp.float32),
        ),
        in_specs=[vmem, smem, vmem, vmem, vmem],
        out_specs=(vmem, vmem),
        compiler_params=pltpu.CompilerParams(vmem_limit_bytes=VMEM_LIMIT),
        name="encode",
    )(
        incidence.reshape(tiles, cap, corners, width),
        live_counts.reshape(1, tiles),
        lame_first.reshape(tiles, cap),
        shear_modulus.reshape(tiles, cap),
        stretch.reshape(3, tiles, cap),
    )
    parts = lax.all_to_all(parts, AXES, 0, 0, tiled=True)
    block_shape = jax.ShapeDtypeStruct((3, 3, width, width), jnp.float32)
    cost = pl.CostEstimate(
        flops=2 * 18 * width * width * lanes * depth, bytes_accessed=10**6, transcendentals=0
    )
    if depth == 2:
        other = lax.ppermute(payload, "gz", [(0, 1), (1, 0)])
        block = pl.pallas_call(
            functools.partial(pair_kernel, cap),
            out_shape=block_shape,
            in_specs=[vmem, vmem],
            out_specs=vmem,
            cost_estimate=cost,
            compiler_params=pltpu.CompilerParams(vmem_limit_bytes=VMEM_LIMIT),
            name="assemble",
        )(payload, other)
    else:
        gathered = lax.all_to_all(payload, "gz", 0, 0, tiled=True)
        block = pl.pallas_call(
            functools.partial(many_kernel, cap),
            out_shape=block_shape,
            in_specs=[vmem],
            out_specs=vmem,
            cost_estimate=cost,
            compiler_params=pltpu.CompilerParams(vmem_limit_bytes=VMEM_LIMIT),
            name="assemble",
        )(gathered)
    entries = 3 * width * lax.axis_size("gx") * lax.axis_size("gy") * tiles
    out = pl.pallas_call(
        functools.partial(scale_kernel, float(entries)),
        out_shape=block_shape,
        in_specs=[vmem, vmem],
        out_specs=anywhere,
        scratch_shapes=[
            pltpu.VMEM((3, 3, width, width), jnp.float32),
            pltpu.SemaphoreType.DMA((3, 3)),
        ],
        compiler_params=pltpu.CompilerParams(vmem_limit_bytes=VMEM_LIMIT),
        name="scale",
    )(parts, block)
    return jnp.transpose(out, (0, 2, 1, 3)).reshape(1, 1, 1, 3, width, 3, width)


def solution(mesh):
    return jax.shard_map(
        on_device,
        mesh=mesh,
        in_specs=(
            P("gx", "gy", "gz", None, None, None, None),
            P("gx", "gy", "gz", None),
            P("gx", "gy", "gz", None, None),
            P("gx", "gy", "gz", None, None),
            P(None, "gx", "gy", "gz", None, None),
        ),
        out_specs=P("gx", "gy", "gz", None, None, None, None),
        check_vma=False,
    )
```

time: 66.8 us -> 18.6 us (0.28)
  blocking collectives: 40.2 us -> 0 us
  other arithmetic: 5.81 us -> 0 us
  Pallas kernels: 0 us -> 3.08 us
  matrix products: 2.72 us -> 0 us
  local copies, waits for them, and re-layouts: 3.6 us -> 1.61 us
  starting transfers between devices: 7.49 us -> 9.16 us
  waiting for transfers between devices: 5.58 us -> 4.54 us
  between operations: 0.74 us -> 0.02 us
    psum x1 -> x0, blocking collectives: 40.2 us -> none  [on_device(): grand_total = lax.psum(diag_sum, ('gx', 'gy', 'gz'))]
    pallas_call x0 -> x3, Pallas kernels: none -> 3.08 us  [the longest x1 1.38 us: on_device(): pl.pallas_call(encode_kernel, out_shape=(jax.ShapeDtypeStruct((devices, l...]
    reduce_sum x3 -> x0, other arithmetic: 3.01 us -> none  [the longest x1 1.59 us: on_device(): position = jnp.sum(onehot * node_iota, axis=3)]
    all_to_all x2 -> x1, waiting for transfers between devices: 5.58 us -> 2.64 us  [on_device(): parts = lax.all_to_all(parts, AXES, 0, 0, tiled=True)]
    dot_general x4 -> x0, matrix products: 2.72 us -> none  [the longest x2 1.37 us: assemble_block(): jnp.einsum('epa,epijb->iajb', onehot, spread, precision=lax.Precision.HIG...]
    ppermute x0 -> x1, waiting for transfers between devices: none -> 1.89 us  [on_device(): other = lax.ppermute(payload, 'gz', [(0, 1), (1, 0)])]
    ppermute x0 -> x1, starting transfers between devices: none -> 1.83 us  [on_device(): other = lax.ppermute(payload, 'gz', [(0, 1), (1, 0)])]
    reshape x1 -> x0, other arithmetic: 0.87 us -> none  [on_device(): (tile_block / mean_diag).reshape(1, 1, 1, 3, tile_width, 3, tile_width)]
  transfers between devices with their start and end apart: 2 -> 2, of which waited for: 2 -> 2; matrix products, arithmetic and copies ran while one was open for 3% -> 0% of each run, Pallas kernels for 0% -> 4%
where the time goes in v1:
time: 18.6 us; the launch traced here: 18.4 us
  starting transfers between devices  9.16 us (49%)
  waiting for transfers between devices  4.54 us (24%)
  Pallas kernels  3.08 us (17%)
  local copies, waits for them, and re-layouts  1.61 us (9%)
    all_to_all x1, starting transfers between devices, on_device(): parts = lax.all_to_all(parts, AXES, 0, 0, tiled=True)  7.33 us
    all_to_all x1, waiting for transfers between devices, on_device(): parts = lax.all_to_all(parts, AXES, 0, 0, tiled=True)  2.64 us
    ppermute x1, waiting for transfers between devices, on_device(): other = lax.ppermute(payload, 'gz', [(0, 1), (1, 0)])  1.89 us
    ppermute x1, starting transfers between devices, on_device(): other = lax.ppermute(payload, 'gz', [(0, 1), (1, 0)])  1.83 us
    unnamed x10, local copies, waits for them, and re-layouts  1.61 us
    pallas_call x1, Pallas kernels, on_device(): pl.pallas_call(encode_kernel, out_shape=(jax.ShapeDtypeStruct((devices, l...  1.38 us
    pallas_call x1, Pallas kernels, on_device(): pl.pallas_call(functools.partial(scale_kernel, float(entries)), out_shape...  1.01 us
    pallas_call x1, Pallas kernels, on_device(): pl.pallas_call(functools.partial(pair_kernel, cap), out_shape=block_shape...  0.69 us
  transfers between devices with their start and end apart: 2, of which 2 were waited for; matrix products, arithmetic and copies ran while one was open for 0% of the time, Pallas kernels for 4%

profile of v1, /device:TPU:0, one launch (start us, length us, event | category | flops | bytes accessed | tf_op | source)
XLA Modules:
  0.0 18.4 jit_solution(7105923378089417558)
XLA Ops:
  0.0 0.0 copy-start.1
  0.0 0.0 copy-start.3
  0.0 0.0 copy-start.2
  0.0 0.0 copy-start.4
  0.0 0.7 %copy-done.1 = f32[3,1,1,1,2,16]{5,4,3,2,1,0:T(2,128)S(1)} copy-done((f32[3,1,1,1,2,16]{5,4,3,2,1,0:T(2,128)S(1)}, f32[3,1,1,1,2,16]{5,4,3,2,1,0:T(2,128)}, u32[]{:S(2)}) %copy-start.1) | copy-done | bytes 408
  0.7 0.0 copy-done.3
  0.7 0.0 copy-done.2
  0.7 0.0 copy-done.4
  0.7 0.0 copy-start
  0.7 0.9 %copy-done = s32[1,1,1,2,16,8,128]{6,5,4,3,2,1,0:T(8,128)S(1)} copy-done((s32[1,1,1,2,16,8,128]{6,5,4,3,2,1,0:T(8,128)S(1)}, s32[1,1,1,2,16,8,128]{6,5,4,3,2,1,0:T(8,128)}, u32[]{:S(2)}) %copy-start) | copy-done | bytes 131096
  1.6 1.4 %encode.1 = (f32[32,128]{1,0:T(8,128)}, f32[2,8,128]{2,1,0:T(8,128)S(1)}) custom-call(s32[2,16,8,128]{3,2,1,0:T(8,128)S(1)} %bitcast.12, s32[1,2]{1,0:T(1,128)S(1)} %bitcast.17, f32[2,16]{1,0:T(2,128)S(1)} %bitcast.15, f32[2,16]{1,0:T(2,128)S(1)} %bitcast.16, f32[3,2,16]{2,1,0:T(2,128)S(1)} %bitcast.14), custom_call_target="tpu_custom_call" | custom-call | tf_op jit(solution)/shard_map/encode/pallas_call | solution.py:154
  3.0 7.3 %all-to-all-start = ((f32[32,1,128]{2,1,0:T(1,128)}), f32[32,1,128]{2,1,0:T(1,128)S(1)}, u32[]{:S(2)}, u32[]{:S(2)}) async-start(f32[32,1,128]{2,1,0:T(1,128)} %bitcast.6), calls=%async_computation | async-start | bytes 32768 | tf_op jit(solution)/shard_map/all_to_all | solution.py:171
  10.3 1.8 %collective-permute-start = (f32[2,8,128]{2,1,0:T(8,128)S(1)}, f32[2,8,128]{2,1,0:T(8,128)S(1)}, u32[]{:S(2)}, u32[]{:S(2)}) collective-permute-start(f32[2,8,128]{2,1,0:T(8,128)S(1)} %get-tuple-element.8.own_ref), channel_id=1, source_target_pairs={{0,1},{1,0},{2,3},{3,2},{4,5},{5,4},{6,7},{7,6},{8,9},{9,8},{10,11... | collective-permute-start | bytes 24584 | tf_op jit(solution)/shard_map/ppermute | solution.py:177
  12.2 1.9 %collective-permute-done.other_ref = f32[2,8,128]{2,1,0:T(8,128)S(1)} collective-permute-done((f32[2,8,128]{2,1,0:T(8,128)S(1)}, f32[2,8,128]{2,1,0:T(8,128)S(1)}, u32[]{:S(2)}, u32[]{:S(2)}) %collective-permute-start) | collective-permute-done | bytes 8224 | tf_op jit(solution)/shard_map/ppermute | solution.py:177
  14.1 0.7 %assemble.1.block_ref = f32[3,3,128,128]{3,2,1,0:T(8,128)S(1)} custom-call(f32[2,8,128]{2,1,0:T(8,128)S(1)} %get-tuple-element.8.own_ref, f32[2,8,128]{2,1,0:T(8,128)S(1)} %collective-permute-done.other_ref), custom_call_target="tpu_custom_call" | custom-call | flops 150994944 | bytes 1000000 | tf_op jit(solution)/shard_map/assemble/pallas_call | solution.py:178
  14.8 2.6 %all-to-all-done = f32[32,1,128]{2,1,0:T(1,128)S(1)} async-done(((f32[32,1,128]{2,1,0:T(1,128)}), f32[32,1,128]{2,1,0:T(1,128)S(1)}, u32[]{:S(2)}, u32[]{:S(2)}) %all-to-all-start) | async-done | bytes 16416 | tf_op jit(solution)/shard_map/all_to_all | solution.py:171
  17.4 1.0 %scale.1 = f32[3,3,128,128]{3,2,1,0:T(8,128)} custom-call(f32[32,128]{1,0:T(8,128)S(1)} %bitcast.13, f32[3,3,128,128]{3,2,1,0:T(8,128)S(1)} %assemble.1.block_ref), custom_call_target="tpu_custom_call" | custom-call | tf_op jit(solution)/shard_map/scale/pallas_call | solution.py:199
Async XLA Ops:
  0.0 0.7 %copy-start.1 = (f32[3,1,1,1,2,16]{5,4,3,2,1,0:T(2,128)S(1)}, f32[3,1,1,1,2,16]{5,4,3,2,1,0:T(2,128)}, u32[]{:S(2)}) copy-start(f32[3,1,1,1,2,16]{5,4,3,2,1,0:T(2,128)} %param.9) | copy-start | bytes 1156
  0.0 0.7 %copy-start.3 = (f32[1,1,1,2,16]{4,3,2,1,0:T(2,128)S(1)}, f32[1,1,1,2,16]{4,3,2,1,0:T(2,128)}, u32[]{:S(2)}) copy-start(f32[1,1,1,2,16]{4,3,2,1,0:T(2,128)} %param.8) | copy-start | bytes 388
  0.0 0.7 %copy-start.2 = (f32[1,1,1,2,16]{4,3,2,1,0:T(2,128)S(1)}, f32[1,1,1,2,16]{4,3,2,1,0:T(2,128)}, u32[]{:S(2)}) copy-start(f32[1,1,1,2,16]{4,3,2,1,0:T(2,128)} %param.7) | copy-start | bytes 388
  0.0 0.7 %copy-start.4 = (s32[1,1,1,2]{3,2,1,0:T(1,128)S(1)}, s32[1,1,1,2]{3,2,1,0:T(1,128)}, u32[]{:S(2)}) copy-start(s32[1,1,1,2]{3,2,1,0:T(1,128)} %param.6) | copy-start | bytes 28
  0.7 0.9 %copy-start = (s32[1,1,1,2,16,8,128]{6,5,4,3,2,1,0:T(8,128)S(1)}, s32[1,1,1,2,16,8,128]{6,5,4,3,2,1,0:T(8,128)}, u32[]{:S(2)}) copy-start(s32[1,1,1,2,16,8,128]{6,5,4,3,2,1,0:T(8,128)} %param.5) | copy-start | bytes 393220
  3.0 14.4 %all-to-all-start = ((f32[32,1,128]{2,1,0:T(1,128)}), f32[32,1,128]{2,1,0:T(1,128)S(1)}, u32[]{:S(2)}, u32[]{:S(2)}) async-start(f32[32,1,128]{2,1,0:T(1,128)} %bitcast.6), calls=%async_computation | async-start | bytes 32768 | tf_op jit(solution)/shard_map/all_to_all | solution.py:171
  10.3 3.7 %collective-permute-start = (f32[2,8,128]{2,1,0:T(8,128)S(1)}, f32[2,8,128]{2,1,0:T(8,128)S(1)}, u32[]{:S(2)}, u32[]{:S(2)}) collective-permute-start(f32[2,8,128]{2,1,0:T(8,128)S(1)} %get-tuple-element.8.own_ref), channel_id=1, source_target_pairs={{0,1},{1,0},{2,3},{3,2},{4,5},{5,4},{6,7},{7,6},{8,9},{9,8},{10,11... | collective-permute-start | bytes 24584 | tf_op jit(solution)/shard_map/ppermute | solution.py:177

commit v2 on v1

v2 whole, which is shorter than its diff:
```python
import math

import jax
import jax.numpy as jnp
from jax import lax
from jax.experimental import pallas as pl
from jax.experimental.pallas import tpu as pltpu
from jax.sharding import PartitionSpec as P

AXES = ("gx", "gy", "gz")
VMEM_LIMIT = 16 * 2**20
FIELDS = 8
DIAGONAL = 2.0 / 9.0


def last_contraction(left, right):
    return lax.dot_general(
        left, right, (((1,), (1,)), ((), ())), preferred_element_type=jnp.float32
    )


def whole(space):
    return pl.BlockSpec(memory_space=space)


def encode_kernel(
    targets, inc_hbm, live_hbm, lame_hbm, shear_hbm, stretch_hbm, pay_ref,
    inc_ref, live_ref, params_ref, inc_done, small_done,
):
    tiles, cap, corners, width = inc_ref.shape
    lanes = corners * cap
    small = [
        pltpu.make_async_copy(live_hbm, live_ref, small_done.at[0]),
        pltpu.make_async_copy(lame_hbm, params_ref.at[0], small_done.at[1]),
        pltpu.make_async_copy(shear_hbm, params_ref.at[1], small_done.at[2]),
        pltpu.make_async_copy(stretch_hbm, params_ref.at[2:5], small_done.at[3]),
    ]
    large = [
        pltpu.make_async_copy(inc_hbm.at[t], inc_ref.at[t], inc_done.at[t]) for t in range(tiles)
    ]
    for copy in large + small:
        copy.start()
    row = lax.broadcasted_iota(jnp.int32, (8, width), 0)
    node = lax.broadcasted_iota(jnp.int32, (8, width), 1)
    reader = jnp.where(row == 0, node, (row == 1).astype(jnp.int32))
    reader = reader.astype(jnp.float32).astype(jnp.bfloat16)
    slot = lax.broadcasted_iota(jnp.int32, (1, lanes), 1) % cap
    for copy in small:
        copy.wait()
    lame, shear = params_ref[0], params_ref[1]
    lengths = [params_ref[2 + k] for k in range(3)]
    inverse = [2.0 / length for length in lengths]
    squares = inverse[0] * inverse[0] + inverse[1] * inverse[1] + inverse[2] * inverse[2]
    volume = lengths[0] * lengths[1] * lengths[2] / 8.0
    weight = volume * (lame + 4.0 * shear) * squares * DIAGONAL
    partial = jnp.zeros((1, cap), jnp.float32)
    node_ids = []
    for t in range(tiles):
        large[t].wait()
        onehot = jnp.concatenate([inc_ref[t, :, p, :] for p in range(corners)], axis=0)
        found = last_contraction(reader, onehot.astype(jnp.float32).astype(jnp.bfloat16))
        here = (found[1:2] > 0.5) & (slot < live_ref[:, t : t + 1])
        node_ids.append(jnp.where(here, found[0:1], -1.0))
        count = here.astype(jnp.float32)
        step = lanes
        while step > cap:
            step //= 2
            count = count + pltpu.roll(count, step, axis=1)
        partial = partial + weight[t : t + 1] * count[:, :cap]
    for t in range(tiles):
        fields = [length[t : t + 1] for length in lengths[::-1]]
        fields += [shear[t : t + 1], lame[t : t + 1]]
        unused = jnp.zeros((FIELDS - 1 - len(fields), cap), jnp.float32)
        fields = jnp.concatenate([partial, unused, *fields], axis=0)
        fields = jnp.concatenate([fields, jnp.zeros((FIELDS, lanes - cap), jnp.float32)], axis=1)
        fields = pltpu.roll(fields, 0, axis=1, stride=cap, stride_axis=0)
        fields = jnp.sum(fields, axis=0, keepdims=True)
        both = jnp.concatenate([node_ids[t], fields], axis=0)
        for member, target in enumerate(targets):
            if target == t:
                pay_ref[member] = both


def walsh(cap, lanes, mask):
    line = lax.broadcasted_iota(jnp.int32, (lanes, lanes), 0)
    column = lax.broadcasted_iota(jnp.int32, (lanes, lanes), 1)
    odd = (column // cap ^ mask) & ~(line // cap)
    odd = (odd ^ odd >> 1 ^ odd >> 2) & 1
    signs = jnp.where(line % cap == column % cap, 1 - 2 * odd, 0)
    return signs.astype(jnp.float32).astype(jnp.bfloat16)


def assemble_kernel(depth, cap, place, pay_ref, block_ref):
    width = block_ref.shape[2]
    lanes = pay_ref.shape[2]
    lane = lax.broadcasted_iota(jnp.int32, (1, lanes), 1)
    mode = lane // cap
    bits = [mode >> k & 1 for k in range(3)]
    thirds = [jnp.where(bit == 1, 1.0 / 3.0, 1.0) for bit in bits]
    masks = {(0, 1): 3, (0, 2): 5, (1, 2): 6}
    tables = {mask: walsh(cap, lanes, mask) for mask in (0, 3, 5, 6)}
    node = lax.broadcasted_iota(jnp.int32, (width, lanes), 0).astype(jnp.float32)
    start = place()
    high, low, right = {}, {}, {mask: [] for mask in tables}
    for source in range(depth):
        payload = pay_ref[start + source]
        fields = jnp.broadcast_to(payload[1:2], (FIELDS, lanes))
        fields = pltpu.roll(fields, 0, axis=1, stride=cap, stride_axis=0)
        fields = jnp.where(lane < cap, fields, 0.0)
        step = cap
        while step < lanes:
            fields = fields + pltpu.roll(fields, step, axis=1)
            step *= 2
        lame, shear = fields[1:2], fields[2:3]
        lengths = [fields[3 + k : 4 + k] for k in range(3)]
        onehot = (node == payload[0:1]).astype(jnp.float32).astype(jnp.bfloat16)
        modes = {
            mask: jnp.dot(onehot, table, preferred_element_type=jnp.float32)
            for mask, table in tables.items()
        }
        for mask in tables:
            right[mask].append(modes[mask].astype(jnp.bfloat16))
        inverse = [2.0 / length for length in lengths]
        scale = lengths[0] * lengths[1] * lengths[2] / 64.0
        squares = []
        for k in range(3):
            others = thirds[(k + 1) % 3] * thirds[(k + 2) % 3]
            squares.append(jnp.where(bits[k] == 1, others, 0.0) * inverse[k] * inverse[k])
        trace = shear * (squares[0] + squares[1] + squares[2])
        for i in range(3):
            for j in range(3):
                if i == j:
                    factor = scale * ((lame + shear) * squares[i] + trace)
                else:
                    material = jnp.where(bits[i] == 1, lame, shear)
                    factor = scale * inverse[i] * inverse[j] * thirds[3 - i - j] * material
                    factor = jnp.where(bits[i] != bits[j], factor, 0.0)
                weighted = modes[0] * factor
                top = weighted.astype(jnp.bfloat16)
                rest = (weighted - top.astype(jnp.float32)).astype(jnp.bfloat16)
                high.setdefault((i, j), []).append(top)
                low.setdefault((i, j), []).append(rest)
    for mask in right:
        right[mask] = jnp.concatenate(right[mask], axis=1)
    for i in range(3):
        for j in range(3):
            other = right[masks[min(i, j), max(i, j)] if i != j else 0]
            block_ref[i, j] = last_contraction(
                jnp.concatenate(high[i, j], axis=1), other
            ) + last_contraction(jnp.concatenate(low[i, j], axis=1), other)


def scale_kernel(entries, cap, parts_ref, swapped_ref, block_ref, out_ref, scaled, done):
    mean = jnp.sum((parts_ref[...] + swapped_ref[...])[:, :cap]) / entries
    copies = []
    for i in range(3):
        for j in range(3):
            scaled[i, j] = block_ref[i, j] / mean
            copy = pltpu.make_async_copy(scaled.at[i, j], out_ref.at[i, j], done.at[i, j])
            copy.start()
            copies.append(copy)
    for copy in copies:
        copy.wait()


def call(kernel, name, out_shape, in_specs, out_spec, scratch=(), flops=10**6):
    return pl.pallas_call(
        kernel,
        out_shape=out_shape,
        in_specs=in_specs,
        out_specs=out_spec,
        scratch_shapes=scratch,
        cost_estimate=pl.CostEstimate(flops=flops, bytes_accessed=10**6, transcendentals=0),
        compiler_params=pltpu.CompilerParams(vmem_limit_bytes=VMEM_LIMIT),
        name=name,
    )


def on_device(incidence, live_counts, lame_first, shear_modulus, stretch):
    tiles, cap, corners, width = incidence.shape[3:]
    lanes = corners * cap
    n_gx, n_gy, depth = (lax.axis_size(a) for a in AXES)
    places = range(n_gx * n_gy * depth - 1, -1, -1)
    groups = [[i for i in places if i // (n_gy * depth) % 2 == half] for half in range(2)]
    members = len(groups[0])
    targets = [i % depth for i in groups[0]]

    def place():
        rank = lax.axis_index("gx") // 2 * n_gy + lax.axis_index("gy")
        return members - (rank + 1) * depth

    vmem, hbm = whole(pltpu.VMEM), whole(pltpu.HBM)
    payload = call(
        lambda *refs: encode_kernel(targets, *refs),
        "encode",
        jax.ShapeDtypeStruct((members, 2, lanes), jnp.float32),
        [hbm] * 5,
        vmem,
        [
            pltpu.VMEM((tiles, cap, corners, width), jnp.int32),
            pltpu.VMEM((1, tiles), jnp.int32),
            pltpu.VMEM((5, tiles, cap), jnp.float32),
            pltpu.SemaphoreType.DMA((tiles,)),
            pltpu.SemaphoreType.DMA((4,)),
        ],
    )(
        *(
            pltpu.with_memory_space_constraint(value, pltpu.HBM)
            for value in (
                incidence.reshape(tiles, cap, corners, width),
                live_counts.reshape(1, tiles),
                lame_first.reshape(tiles, cap),
                shear_modulus.reshape(tiles, cap),
                stretch.reshape(3, tiles, cap),
            )
        )
    )
    gathered = lax.all_to_all(payload, AXES, 0, 0, axis_index_groups=groups, tiled=True)
    parts = jnp.sum(gathered[:, 1], axis=0, keepdims=True)
    swapped = lax.ppermute(parts, "gx", [(i, i ^ 1) for i in range(n_gx)])
    block_shape = jax.ShapeDtypeStruct((3, 3, width, width), jnp.float32)
    block = call(
        lambda *refs: assemble_kernel(depth, cap, place, *refs),
        "assemble",
        block_shape,
        [vmem],
        vmem,
        flops=2 * 18 * width * width * lanes * depth,
    )(gathered)
    entries = float(3 * width * n_gx * n_gy * tiles)
    out = call(
        lambda *refs: scale_kernel(entries, cap, *refs),
        "scale",
        block_shape,
        [vmem] * 3,
        hbm,
        [
            pltpu.VMEM((3, 3, width, width), jnp.float32),
            pltpu.SemaphoreType.DMA((3, 3)),
        ],
    )(parts, swapped, block)
    return jnp.transpose(out, (0, 2, 1, 3)).reshape(1, 1, 1, 3, width, 3, width)


def solution(mesh):
    return jax.shard_map(
        on_device,
        mesh=mesh,
        in_specs=(
            P("gx", "gy", "gz", None, None, None, None),
            P("gx", "gy", "gz", None),
            P("gx", "gy", "gz", None, None),
            P("gx", "gy", "gz", None, None),
            P(None, "gx", "gy", "gz", None, None),
        ),
        out_specs=P("gx", "gy", "gz", None, None, None, None),
        check_vma=False,
    )
```

time: 18.6 us -> 16.1 us (0.87)
  blocking collectives: 0 us -> 11.9 us
  starting transfers between devices: 9.16 us -> 0.06 us
  waiting for transfers between devices: 4.54 us -> 0.36 us
  local copies, waits for them, and re-layouts: 1.61 us -> 0 us
  Pallas kernels: 3.08 us -> 3.54 us
    all_to_all x0 -> x1, blocking collectives: none -> 11.9 us  [on_device(): lax.all_to_all(payload, AXES, 0, 0, axis_index_groups=groups, tiled=True)]
    all_to_all x1 -> x0, starting transfers between devices: 7.33 us -> none  [on_device(): parts = lax.all_to_all(parts, AXES, 0, 0, tiled=True)]
    all_to_all x1 -> x0, waiting for transfers between devices: 2.64 us -> none  [on_device(): parts = lax.all_to_all(parts, AXES, 0, 0, tiled=True)]
    ppermute x1, starting transfers between devices: 1.83 us -> 0.06 us  [on_device(): swapped = lax.ppermute(parts, 'gx', [(i, i ^ 1) for i in range(n_gx)])]
    unnamed x10 -> x0, local copies, waits for them, and re-layouts: 1.61 us -> none
    ppermute x1, waiting for transfers between devices: 1.89 us -> 0.36 us  [on_device(): swapped = lax.ppermute(parts, 'gx', [(i, i ^ 1) for i in range(n_gx)])]
    pallas_call x3, Pallas kernels: 3.08 us -> 3.54 us  [the longest x1 1.75 us: on_device(): call(lambda *refs: encode_kernel(targets, *refs), 'encode', jax.ShapeDtyp...]
  transfers between devices with their start and end apart: 2 -> 1, of which waited for: 2 -> 1; matrix products, arithmetic and copies ran while one was open for 0% -> 0% of each run, Pallas kernels for 4% -> 5%
where the time goes in v2:
time: 16.1 us; the launch traced here: 15.9 us
  blocking collectives  11.9 us (74%)
  Pallas kernels  3.54 us (22%)
  waiting for transfers between devices  0.36 us (2%)
    all_to_all x1, blocking collectives, on_device(): lax.all_to_all(payload, AXES, 0, 0, axis_index_groups=groups, tiled=True)  11.9 us
    pallas_call x1, Pallas kernels, on_device(): call(lambda *refs: encode_kernel(targets, *refs), 'encode', jax.ShapeDtyp...  1.75 us
    pallas_call x1, Pallas kernels, on_device(): call(lambda *refs: scale_kernel(entries, cap, *refs), 'scale', block_shap...  1.01 us
    pallas_call x1, Pallas kernels, on_device(): call(lambda *refs: assemble_kernel(depth, cap, place, *refs), 'assemble',...  0.78 us
    ppermute x1, waiting for transfers between devices, on_device(): swapped = lax.ppermute(parts, 'gx', [(i, i ^ 1) for i in range(n_gx)])  0.36 us
  transfers between devices with their start and end apart: 1, of which 1 were waited for; matrix products, arithmetic and copies ran while one was open for 0% of the time, Pallas kernels for 5%

profile of v2, /device:TPU:0, one launch (start us, length us, event | category | flops | bytes accessed | tf_op | source)
XLA Modules:
  0.0 15.9 jit_solution(14689191993044640047)
XLA Ops:
  0.0 1.8 %encode.1 = f32[16,2,128]{2,1,0:T(2,128)S(1)} custom-call(s32[2,16,8,128]{3,2,1,0:T(8,128)} %bitcast.11, s32[1,2]{1,0:T(1,128)} %bitcast.15, f32[2,16]{1,0:T(2,128)} %bitcast.13, f32[2,16]{1,0:T(2,128)} %bitcast.14, f32[3,2,16]{2,1,0:T(2,128)} %bitcast.12), custom_call_target="tpu_custom_call" | custom-call | flops 1000000 | bytes 1000000 | tf_op jit(solution)/shard_map/encode/pallas_call | solution.py:193
  1.8 11.9 %all_to_all.5.refs_0_ = f32[16,2,128]{2,1,0:T(2,128)S(1)} all-to-all(f32[16,2,128]{2,1,0:T(2,128)S(1)} %encode.1), channel_id=1, replica_groups={{23,22,21,20,19,18,17,16,7,6,5,4,3,2,1,0},{31,30,29,28,27,26,25,24,15,1..., dimensions={0} | all-to-all | bytes 32768 | tf_op jit(solution)/shard_map/all_to_all | solution.py:218
  13.7 0.1 collective-permute-start
  13.7 0.8 %assemble.1.refs_2_ = f32[3,3,128,128]{3,2,1,0:T(8,128)S(1)} custom-call(f32[16,2,128]{2,1,0:T(2,128)S(1)} %all_to_all.5.refs_0_), custom_call_target="tpu_custom_call" | custom-call | flops 150994944 | bytes 1000000 | tf_op jit(solution)/shard_map/assemble/pallas_call | solution.py:222
  14.5 0.4 %collective-permute-done.refs_1_ = f32[1,128]{1,0:T(1,128)S(1)} collective-permute-done((f32[1,128]{1,0:T(1,128)S(1)}, f32[1,128]{1,0:T(1,128)S(1)}, u32[]{:S(2)}, u32[]{:S(2)}) %collective-permute-start) | collective-permute-done | bytes 544 | tf_op jit(solution)/shard_map/ppermute | solution.py:220
  14.9 1.0 %scale.1 = f32[3,3,128,128]{3,2,1,0:T(8,128)} custom-call(f32[1,128]{1,0:T(1,128)S(1)} %bitcast.10, f32[1,128]{1,0:T(1,128)S(1)} %collective-permute-done.refs_1_, f32[3,3,128,128]{3,2,1,0:T(8,128)S(1)} %assemble.1.refs_2_), custom_call_target="tpu_custom_call" | custom-call | flops 1000000 | bytes 1000000 | tf_op jit(solution)/shard_map/scale/pallas_call | solution.py:231
  (1 shorter events, 0.0 us)
Async XLA Ops:
  13.7 1.2 %collective-permute-start = (f32[1,128]{1,0:T(1,128)S(1)}, f32[1,128]{1,0:T(1,128)S(1)}, u32[]{:S(2)}, u32[]{:S(2)}) collective-permute-start(f32[1,128]{1,0:T(1,128)S(1)} %bitcast.9), channel_id=1, source_target_pairs={{0,8},{8,0},{16,24},{24,16},{1,9},{9,1},{17,25},{25,17},{2,10},{10... | collective-permute-start | bytes 1544 | tf_op jit(solution)/shard_map/ppermute | solution.py:220

commit v3 on v2

--- a/solution.py
+++ b/solution.py
@@ -9,6 +9,7 @@
 
 AXES = ("gx", "gy", "gz")
 VMEM_LIMIT = 16 * 2**20
+CHUNKS = 2
 FIELDS = 8
 DIAGONAL = 2.0 / 9.0
 
@@ -29,22 +30,30 @@
 ):
     tiles, cap, corners, width = inc_ref.shape
     lanes = corners * cap
+    chunks = inc_done.shape[1]
+    part = cap // chunks
     small = [
         pltpu.make_async_copy(live_hbm, live_ref, small_done.at[0]),
         pltpu.make_async_copy(lame_hbm, params_ref.at[0], small_done.at[1]),
         pltpu.make_async_copy(shear_hbm, params_ref.at[1], small_done.at[2]),
         pltpu.make_async_copy(stretch_hbm, params_ref.at[2:5], small_done.at[3]),
     ]
-    large = [
-        pltpu.make_async_copy(inc_hbm.at[t], inc_ref.at[t], inc_done.at[t]) for t in range(tiles)
-    ]
-    for copy in large + small:
+    large = []
+    for t in range(tiles):
+        for c in range(chunks):
+            slots = pl.ds(c * part, part)
+            large.append(
+                pltpu.make_async_copy(inc_hbm.at[t, slots], inc_ref.at[t, slots], inc_done.at[t, c])
+            )
+    for copy in small + large:
         copy.start()
     row = lax.broadcasted_iota(jnp.int32, (8, width), 0)
     node = lax.broadcasted_iota(jnp.int32, (8, width), 1)
     reader = jnp.where(row == 0, node, (row == 1).astype(jnp.int32))
     reader = reader.astype(jnp.float32).astype(jnp.bfloat16)
-    slot = lax.broadcasted_iota(jnp.int32, (1, lanes), 1) % cap
+    lane = lax.broadcasted_iota(jnp.int32, (1, lanes), 1)
+    line = lax.broadcasted_iota(jnp.int32, (cap, lanes), 0)
+    spread = (line == lax.broadcasted_iota(jnp.int32, (cap, lanes), 1) // corners).astype(jnp.float32)
     for copy in small:
         copy.wait()
     lame, shear = params_ref[0], params_ref[1]
@@ -53,40 +62,47 @@
     squares = inverse[0] * inverse[0] + inverse[1] * inverse[1] + inverse[2] * inverse[2]
     volume = lengths[0] * lengths[1] * lengths[2] / 8.0
     weight = volume * (lame + 4.0 * shear) * squares * DIAGONAL
-    partial = jnp.zeros((1, cap), jnp.float32)
-    node_ids = []
-    for t in range(tiles):
-        large[t].wait()
-        onehot = jnp.concatenate([inc_ref[t, :, p, :] for p in range(corners)], axis=0)
-        found = last_contraction(reader, onehot.astype(jnp.float32).astype(jnp.bfloat16))
-        here = (found[1:2] > 0.5) & (slot < live_ref[:, t : t + 1])
-        node_ids.append(jnp.where(here, found[0:1], -1.0))
-        count = here.astype(jnp.float32)
-        step = lanes
-        while step > cap:
-            step //= 2
-            count = count + pltpu.roll(count, step, axis=1)
-        partial = partial + weight[t : t + 1] * count[:, :cap]
+    weight = jnp.dot(
+        weight, spread, preferred_element_type=jnp.float32, precision=lax.Precision.HIGHEST
+    )
+    field_rows = []
     for t in range(tiles):
         fields = [length[t : t + 1] for length in lengths[::-1]]
         fields += [shear[t : t + 1], lame[t : t + 1]]
-        unused = jnp.zeros((FIELDS - 1 - len(fields), cap), jnp.float32)
-        fields = jnp.concatenate([partial, unused, *fields], axis=0)
+        unused = jnp.zeros((FIELDS - len(fields), cap), jnp.float32)
+        fields = jnp.concatenate([unused, *fields], axis=0)
         fields = jnp.concatenate([fields, jnp.zeros((FIELDS, lanes - cap), jnp.float32)], axis=1)
         fields = pltpu.roll(fields, 0, axis=1, stride=cap, stride_axis=0)
-        fields = jnp.sum(fields, axis=0, keepdims=True)
-        both = jnp.concatenate([node_ids[t], fields], axis=0)
+        field_rows.append(jnp.sum(fields, axis=0, keepdims=True))
+    live = [lane // corners < live_ref[:, t : t + 1] for t in range(tiles)]
+    for copy in large:
+        copy.wait()
+    partial = jnp.zeros((1, lanes), jnp.float32)
+    node_ids = []
+    onehot = inc_ref[...].reshape(tiles * lanes, width)
+    found = last_contraction(reader, onehot.astype(jnp.float32).astype(jnp.bfloat16))
+    for t in range(tiles):
+        position = found[0:1, t * lanes : (t + 1) * lanes]
+        here = (found[1:2, t * lanes : (t + 1) * lanes] > 0.5) & live[t]
+        node_ids.append(jnp.where(here, position, -1.0))
+        partial = partial + jnp.where(here, weight[t : t + 1], 0.0)
+    partial = jnp.sum(partial, axis=1, keepdims=True)
+    for t in range(tiles):
+        both = jnp.concatenate(
+            [node_ids[t], jnp.where(lane == 0, partial, field_rows[t])], axis=0
+        )
         for member, target in enumerate(targets):
             if target == t:
                 pay_ref[member] = both
 
 
 def walsh(cap, lanes, mask):
+    corners = lanes // cap
     line = lax.broadcasted_iota(jnp.int32, (lanes, lanes), 0)
     column = lax.broadcasted_iota(jnp.int32, (lanes, lanes), 1)
-    odd = (column // cap ^ mask) & ~(line // cap)
+    odd = (column // cap ^ mask) & ~(line % corners)
     odd = (odd ^ odd >> 1 ^ odd >> 2) & 1
-    signs = jnp.where(line % cap == column % cap, 1 - 2 * odd, 0)
+    signs = jnp.where(line // corners == column % cap, 1 - 2 * odd, 0)
     return signs.astype(jnp.float32).astype(jnp.bfloat16)
 
 
@@ -150,12 +166,13 @@
             ) + last_contraction(jnp.concatenate(low[i, j], axis=1), other)
 
 
-def scale_kernel(entries, cap, parts_ref, swapped_ref, block_ref, out_ref, scaled, done):
-    mean = jnp.sum((parts_ref[...] + swapped_ref[...])[:, :cap]) / entries
+def scale_kernel(entries, parts_ref, swapped_ref, block_ref, out_ref, scaled, done):
+    mean = (parts_ref[...] + swapped_ref[...])[:, :1] / entries
+    inverse = 1.0 / mean
     copies = []
     for i in range(3):
         for j in range(3):
-            scaled[i, j] = block_ref[i, j] / mean
+            scaled[i, j] = block_ref[i, j] * inverse
             copy = pltpu.make_async_copy(scaled.at[i, j], out_ref.at[i, j], done.at[i, j])
             copy.start()
             copies.append(copy)
@@ -200,7 +217,7 @@
             pltpu.VMEM((tiles, cap, corners, width), jnp.int32),
             pltpu.VMEM((1, tiles), jnp.int32),
             pltpu.VMEM((5, tiles, cap), jnp.float32),
-            pltpu.SemaphoreType.DMA((tiles,)),
+            pltpu.SemaphoreType.DMA((tiles, CHUNKS)),
             pltpu.SemaphoreType.DMA((4,)),
         ],
     )(
@@ -229,7 +246,7 @@
     )(gathered)
     entries = float(3 * width * n_gx * n_gy * tiles)
     out = call(
-        lambda *refs: scale_kernel(entries, cap, *refs),
+        lambda *refs: scale_kernel(entries, *refs),
         "scale",
         block_shape,
         [vmem] * 3,

time: 16.1 us -> 15.5 us (0.963)
  Pallas kernels: 3.54 us -> 2.98 us
    pallas_call x1, Pallas kernels: 1.75 us -> 1.24 us  [on_device(): call(lambda *refs: encode_kernel(targets, *refs), 'encode', jax.ShapeDtyp...]
where the time goes in v3:
time: 15.5 us; the launch traced here: 15.3 us
  blocking collectives  11.9 us (77%)
  Pallas kernels  2.98 us (19%)
  waiting for transfers between devices  0.36 us (2%)
    all_to_all x1, blocking collectives, on_device(): lax.all_to_all(payload, AXES, 0, 0, axis_index_groups=groups, tiled=True)  11.9 us
    pallas_call x1, Pallas kernels, on_device(): call(lambda *refs: encode_kernel(targets, *refs), 'encode', jax.ShapeDtyp...  1.24 us
    pallas_call x1, Pallas kernels, on_device(): call(lambda *refs: scale_kernel(entries, *refs), 'scale', block_shape, [v...  0.96 us
    pallas_call x1, Pallas kernels, on_device(): call(lambda *refs: assemble_kernel(depth, cap, place, *refs), 'assemble',...  0.78 us
    ppermute x1, waiting for transfers between devices, on_device(): swapped = lax.ppermute(parts, 'gx', [(i, i ^ 1) for i in range(n_gx)])  0.36 us
  transfers between devices with their start and end apart: 1, of which 1 were waited for; matrix products, arithmetic and copies ran while one was open for 0% of the time, Pallas kernels for 5%

profile of v3, /device:TPU:0, one launch (start us, length us, event | category | flops | bytes accessed | tf_op | source)
XLA Modules:
  0.0 15.3 jit_solution(2391112670411886417)
XLA Ops:
  0.0 1.2 %encode.1 = f32[16,2,128]{2,1,0:T(2,128)S(1)} custom-call(s32[2,16,8,128]{3,2,1,0:T(8,128)} %bitcast.11, s32[1,2]{1,0:T(1,128)} %bitcast.15, f32[2,16]{1,0:T(2,128)} %bitcast.13, f32[2,16]{1,0:T(2,128)} %bitcast.14, f32[3,2,16]{2,1,0:T(2,128)} %bitcast.12), custom_call_target="tpu_custom_call" | custom-call | flops 1000000 | bytes 1000000 | tf_op jit(solution)/shard_map/encode/pallas_call | solution.py:210
  1.2 11.9 %all_to_all.5.refs_0_ = f32[16,2,128]{2,1,0:T(2,128)S(1)} all-to-all(f32[16,2,128]{2,1,0:T(2,128)S(1)} %encode.1), channel_id=1, replica_groups={{23,22,21,20,19,18,17,16,7,6,5,4,3,2,1,0},{31,30,29,28,27,26,25,24,15,1..., dimensions={0} | all-to-all | bytes 32768 | tf_op jit(solution)/shard_map/all_to_all | solution.py:235
  13.1 0.1 collective-permute-start
  13.2 0.8 %assemble.1.refs_2_ = f32[3,3,128,128]{3,2,1,0:T(8,128)S(1)} custom-call(f32[16,2,128]{2,1,0:T(2,128)S(1)} %all_to_all.5.refs_0_), custom_call_target="tpu_custom_call" | custom-call | flops 150994944 | bytes 1000000 | tf_op jit(solution)/shard_map/assemble/pallas_call | solution.py:239
  14.0 0.4 %collective-permute-done.refs_1_ = f32[1,128]{1,0:T(1,128)S(1)} collective-permute-done((f32[1,128]{1,0:T(1,128)S(1)}, f32[1,128]{1,0:T(1,128)S(1)}, u32[]{:S(2)}, u32[]{:S(2)}) %collective-permute-start) | collective-permute-done | bytes 544 | tf_op jit(solution)/shard_map/ppermute | solution.py:237
  14.4 1.0 %scale.1 = f32[3,3,128,128]{3,2,1,0:T(8,128)} custom-call(f32[1,128]{1,0:T(1,128)S(1)} %bitcast.10, f32[1,128]{1,0:T(1,128)S(1)} %collective-permute-done.refs_1_, f32[3,3,128,128]{3,2,1,0:T(8,128)S(1)} %assemble.1.refs_2_), custom_call_target="tpu_custom_call" | custom-call | flops 1000000 | bytes 1000000 | tf_op jit(solution)/shard_map/scale/pallas_call | solution.py:248
  (1 shorter events, 0.0 us)
Async XLA Ops:
  13.1 1.2 %collective-permute-start = (f32[1,128]{1,0:T(1,128)S(1)}, f32[1,128]{1,0:T(1,128)S(1)}, u32[]{:S(2)}, u32[]{:S(2)}) collective-permute-start(f32[1,128]{1,0:T(1,128)S(1)} %bitcast.9), channel_id=1, source_target_pairs={{0,8},{8,0},{16,24},{24,16},{1,9},{9,1},{17,25},{25,17},{2,10},{10... | collective-permute-start | bytes 1544 | tf_op jit(solution)/shard_map/ppermute | solution.py:237

commit v4 on v3

--- a/solution.py
+++ b/solution.py
@@ -9,7 +9,7 @@
 
 AXES = ("gx", "gy", "gz")
 VMEM_LIMIT = 16 * 2**20
-CHUNKS = 2
+CUTS = (0, 3, 6, 9)
 FIELDS = 8
 DIAGONAL = 2.0 / 9.0
 
@@ -30,22 +30,14 @@
 ):
     tiles, cap, corners, width = inc_ref.shape
     lanes = corners * cap
-    chunks = inc_done.shape[1]
-    part = cap // chunks
     small = [
         pltpu.make_async_copy(live_hbm, live_ref, small_done.at[0]),
         pltpu.make_async_copy(lame_hbm, params_ref.at[0], small_done.at[1]),
         pltpu.make_async_copy(shear_hbm, params_ref.at[1], small_done.at[2]),
         pltpu.make_async_copy(stretch_hbm, params_ref.at[2:5], small_done.at[3]),
     ]
-    large = []
-    for t in range(tiles):
-        for c in range(chunks):
-            slots = pl.ds(c * part, part)
-            large.append(
-                pltpu.make_async_copy(inc_hbm.at[t, slots], inc_ref.at[t, slots], inc_done.at[t, c])
-            )
-    for copy in small + large:
+    large = pltpu.make_async_copy(inc_hbm, inc_ref, inc_done)
+    for copy in [large, *small]:
         copy.start()
     row = lax.broadcasted_iota(jnp.int32, (8, width), 0)
     node = lax.broadcasted_iota(jnp.int32, (8, width), 1)
@@ -75,8 +67,7 @@
         fields = pltpu.roll(fields, 0, axis=1, stride=cap, stride_axis=0)
         field_rows.append(jnp.sum(fields, axis=0, keepdims=True))
     live = [lane // corners < live_ref[:, t : t + 1] for t in range(tiles)]
-    for copy in large:
-        copy.wait()
+    large.wait()
     partial = jnp.zeros((1, lanes), jnp.float32)
     node_ids = []
     onehot = inc_ref[...].reshape(tiles * lanes, width)
@@ -107,7 +98,7 @@
 
 
 def assemble_kernel(depth, cap, place, pay_ref, block_ref):
-    width = block_ref.shape[2]
+    width = block_ref.shape[1]
     lanes = pay_ref.shape[2]
     lane = lax.broadcasted_iota(jnp.int32, (1, lanes), 1)
     mode = lane // cap
@@ -161,7 +152,7 @@
     for i in range(3):
         for j in range(3):
             other = right[masks[min(i, j), max(i, j)] if i != j else 0]
-            block_ref[i, j] = last_contraction(
+            block_ref[3 * i + j] = last_contraction(
                 jnp.concatenate(high[i, j], axis=1), other
             ) + last_contraction(jnp.concatenate(low[i, j], axis=1), other)
 
@@ -170,12 +161,12 @@
     mean = (parts_ref[...] + swapped_ref[...])[:, :1] / entries
     inverse = 1.0 / mean
     copies = []
-    for i in range(3):
-        for j in range(3):
-            scaled[i, j] = block_ref[i, j] * inverse
-            copy = pltpu.make_async_copy(scaled.at[i, j], out_ref.at[i, j], done.at[i, j])
-            copy.start()
-            copies.append(copy)
+    for n, (first, last) in enumerate(zip(CUTS[:-1], CUTS[1:])):
+        part = pl.ds(first, last - first)
+        scaled[part] = block_ref[part] * inverse
+        copy = pltpu.make_async_copy(scaled.at[part], out_ref.at[part], done.at[n])
+        copy.start()
+        copies.append(copy)
     for copy in copies:
         copy.wait()
 
@@ -198,7 +189,8 @@
     lanes = corners * cap
     n_gx, n_gy, depth = (lax.axis_size(a) for a in AXES)
     places = range(n_gx * n_gy * depth - 1, -1, -1)
-    groups = [[i for i in places if i // (n_gy * depth) % 2 == half] for half in range(2)]
+    turn = [(g ^ g >> 1) & 1 for g in range(n_gx)]
+    groups = [[i for i in places if turn[i // (n_gy * depth)] == half] for half in range(2)]
     members = len(groups[0])
     targets = [i % depth for i in groups[0]]
 
@@ -217,7 +209,7 @@
             pltpu.VMEM((tiles, cap, corners, width), jnp.int32),
             pltpu.VMEM((1, tiles), jnp.int32),
             pltpu.VMEM((5, tiles, cap), jnp.float32),
-            pltpu.SemaphoreType.DMA((tiles, CHUNKS)),
+            pltpu.SemaphoreType.DMA,
             pltpu.SemaphoreType.DMA((4,)),
         ],
     )(
@@ -235,7 +227,7 @@
     gathered = lax.all_to_all(payload, AXES, 0, 0, axis_index_groups=groups, tiled=True)
     parts = jnp.sum(gathered[:, 1], axis=0, keepdims=True)
     swapped = lax.ppermute(parts, "gx", [(i, i ^ 1) for i in range(n_gx)])
-    block_shape = jax.ShapeDtypeStruct((3, 3, width, width), jnp.float32)
+    block_shape = jax.ShapeDtypeStruct((9, width, width), jnp.float32)
     block = call(
         lambda *refs: assemble_kernel(depth, cap, place, *refs),
         "assemble",
@@ -252,11 +244,12 @@
         [vmem] * 3,
         hbm,
         [
-            pltpu.VMEM((3, 3, width, width), jnp.float32),
-            pltpu.SemaphoreType.DMA((3, 3)),
+            pltpu.VMEM((9, width, width), jnp.float32),
+            pltpu.SemaphoreType.DMA((len(CUTS) - 1,)),
         ],
     )(parts, swapped, block)
-    return jnp.transpose(out, (0, 2, 1, 3)).reshape(1, 1, 1, 3, width, 3, width)
+    out = jnp.transpose(out.reshape(3, 3, width, width), (0, 2, 1, 3))
+    return out.reshape(1, 1, 1, 3, width, 3, width)
 
 
 def solution(mesh):

time: 15.5 us -> 15 us (0.968)
  blocking collectives: 11.9 us -> 11.4 us
  starting transfers between devices: 0.06 us -> 0.26 us
  waiting for transfers between devices: 0.36 us -> 0.17 us
    all_to_all x1, blocking collectives: 11.9 us -> 11.4 us  [on_device(): lax.all_to_all(payload, AXES, 0, 0, axis_index_groups=groups, tiled=True)]
    ppermute x1, starting transfers between devices: 0.06 us -> 0.26 us  [on_device(): swapped = lax.ppermute(parts, 'gx', [(i, i ^ 1) for i in range(n_gx)])]
    ppermute x1, waiting for transfers between devices: 0.36 us -> 0.17 us  [on_device(): swapped = lax.ppermute(parts, 'gx', [(i, i ^ 1) for i in range(n_gx)])]
where the time goes in v4:
time: 15 us; the launch traced here: 14.8 us
  blocking collectives  11.4 us (76%)
  Pallas kernels  2.93 us (20%)
  starting transfers between devices  0.26 us (2%)
  waiting for transfers between devices  0.17 us (1%)
    all_to_all x1, blocking collectives, on_device(): lax.all_to_all(payload, AXES, 0, 0, axis_index_groups=groups, tiled=True)  11.4 us
    pallas_call x1, Pallas kernels, on_device(): call(lambda *refs: encode_kernel(targets, *refs), 'encode', jax.ShapeDtyp...  1.23 us
    pallas_call x1, Pallas kernels, on_device(): call(lambda *refs: scale_kernel(entries, *refs), 'scale', block_shape, [v...  0.92 us
    pallas_call x1, Pallas kernels, on_device(): call(lambda *refs: assemble_kernel(depth, cap, place, *refs), 'assemble',...  0.78 us
  transfers between devices with their start and end apart: 1, of which 1 were waited for; matrix products, arithmetic and copies ran while one was open for 0% of the time, Pallas kernels for 5%

profile of v4, /device:TPU:0, one launch (start us, length us, event | category | flops | bytes accessed | tf_op | source)
XLA Modules:
  0.0 14.8 jit_solution(3509722627329889700)
XLA Ops:
  0.0 1.2 %encode.1 = f32[16,2,128]{2,1,0:T(2,128)S(1)} custom-call(s32[2,16,8,128]{3,2,1,0:T(8,128)} %bitcast.13, s32[1,2]{1,0:T(1,128)} %bitcast.17, f32[2,16]{1,0:T(2,128)} %bitcast.15, f32[2,16]{1,0:T(2,128)} %bitcast.16, f32[3,2,16]{2,1,0:T(2,128)} %bitcast.14), custom_call_target="tpu_custom_call" | custom-call | flops 1000000 | bytes 1000000 | tf_op jit(solution)/shard_map/encode/pallas_call | solution.py:202
  1.2 11.4 %all_to_all.5.refs_0_ = f32[16,2,128]{2,1,0:T(2,128)S(1)} all-to-all(f32[16,2,128]{2,1,0:T(2,128)S(1)} %encode.1), channel_id=1, replica_groups={{31,30,29,28,27,26,25,24,7,6,5,4,3,2,1,0},{23,22,21,20,19,18,17,16,15,1..., dimensions={0} | all-to-all | bytes 32768 | tf_op jit(solution)/shard_map/all_to_all | solution.py:227
  12.7 0.3 %collective-permute-start = (f32[1,128]{1,0:T(1,128)S(1)}, f32[1,128]{1,0:T(1,128)S(1)}, u32[]{:S(2)}, u32[]{:S(2)}) collective-permute-start(f32[1,128]{1,0:T(1,128)S(1)} %bitcast.11), channel_id=1, source_target_pairs={{0,8},{8,0},{16,24},{24,16},{1,9},{9,1},{17,25},{25,17},{2,10},{10... | collective-permute-start | bytes 1544 | tf_op jit(solution)/shard_map/ppermute | solution.py:229
  12.9 0.8 %assemble.1.refs_2_ = f32[9,128,128]{2,1,0:T(8,128)S(1)} custom-call(f32[16,2,128]{2,1,0:T(2,128)S(1)} %all_to_all.5.refs_0_), custom_call_target="tpu_custom_call" | custom-call | flops 150994944 | bytes 1000000 | tf_op jit(solution)/shard_map/assemble/pallas_call | solution.py:231
  13.7 0.2 %collective-permute-done.refs_1_ = f32[1,128]{1,0:T(1,128)S(1)} collective-permute-done((f32[1,128]{1,0:T(1,128)S(1)}, f32[1,128]{1,0:T(1,128)S(1)}, u32[]{:S(2)}, u32[]{:S(2)}) %collective-permute-start) | collective-permute-done | bytes 544 | tf_op jit(solution)/shard_map/ppermute | solution.py:229
  13.9 0.9 %scale.1 = f32[9,128,128]{2,1,0:T(8,128)} custom-call(f32[1,128]{1,0:T(1,128)S(1)} %bitcast.12, f32[1,128]{1,0:T(1,128)S(1)} %collective-permute-done.refs_1_, f32[9,128,128]{2,1,0:T(8,128)S(1)} %assemble.1.refs_2_), custom_call_target="tpu_custom_call" | custom-call | flops 1000000 | bytes 1000000 | tf_op jit(solution)/shard_map/scale/pallas_call | solution.py:240
  (1 shorter events, 0.0 us)
Async XLA Ops:
  12.7 1.2 %collective-permute-start = (f32[1,128]{1,0:T(1,128)S(1)}, f32[1,128]{1,0:T(1,128)S(1)}, u32[]{:S(2)}, u32[]{:S(2)}) collective-permute-start(f32[1,128]{1,0:T(1,128)S(1)} %bitcast.11), channel_id=1, source_target_pairs={{0,8},{8,0},{16,24},{24,16},{1,9},{9,1},{17,25},{25,17},{2,10},{10... | collective-permute-start | bytes 1544 | tf_op jit(solution)/shard_map/ppermute | solution.py:229

commit v5 on v4

--- a/solution.py
+++ b/solution.py
@@ -37,7 +37,13 @@
         pltpu.make_async_copy(stretch_hbm, params_ref.at[2:5], small_done.at[3]),
     ]
     large = pltpu.make_async_copy(inc_hbm, inc_ref, inc_done)
-    for copy in [large, *small]:
+    part = cap // 2
+    pieces = [
+        pltpu.make_async_copy(inc_hbm.at[t, pl.ds(c, part)], inc_ref.at[t, pl.ds(c, part)], inc_done)
+        for t in range(tiles)
+        for c in (0, part)
+    ]
+    for copy in [*pieces[:2], *small, *pieces[2:]]:
         copy.start()
     row = lax.broadcasted_iota(jnp.int32, (8, width), 0)
     node = lax.broadcasted_iota(jnp.int32, (8, width), 1)
@@ -188,9 +194,13 @@
     tiles, cap, corners, width = incidence.shape[3:]
     lanes = corners * cap
     n_gx, n_gy, depth = (lax.axis_size(a) for a in AXES)
-    places = range(n_gx * n_gy * depth - 1, -1, -1)
-    turn = [(g ^ g >> 1) & 1 for g in range(n_gx)]
-    groups = [[i for i in places if turn[i // (n_gy * depth)] == half] for half in range(2)]
+    places = [
+        (2 * k + int(k + h > (n_gx // 2 + n_gy) // 2 - 1), h, z)
+        for k in reversed(range(n_gx // 2))
+        for h in reversed(range(n_gy))
+        for z in reversed(range(depth))
+    ]
+    groups = [[((g ^ half) * n_gy + h) * depth + z for g, h, z in places] for half in range(2)]
     members = len(groups[0])
     targets = [i % depth for i in groups[0]]
 

time: 15 us -> 14.9 us (level)
  no operation moved by 1% of the time
where the time goes in v5:
time: 14.9 us; the launch traced here: 14.7 us
  blocking collectives  11.3 us (76%)
  Pallas kernels  2.91 us (20%)
  starting transfers between devices  0.37 us (2%)
    all_to_all x1, blocking collectives, on_device(): lax.all_to_all(payload, AXES, 0, 0, axis_index_groups=groups, tiled=True)  11.3 us
    pallas_call x1, Pallas kernels, on_device(): call(lambda *refs: encode_kernel(targets, *refs), 'encode', jax.ShapeDtyp...  1.21 us
    pallas_call x1, Pallas kernels, on_device(): call(lambda *refs: scale_kernel(entries, *refs), 'scale', block_shape, [v...  0.92 us
    pallas_call x1, Pallas kernels, on_device(): call(lambda *refs: assemble_kernel(depth, cap, place, *refs), 'assemble',...  0.78 us
    ppermute x1, starting transfers between devices, on_device(): swapped = lax.ppermute(parts, 'gx', [(i, i ^ 1) for i in range(n_gx)])  0.37 us
  transfers between devices with their start and end apart: 1, of which 1 were waited for; matrix products, arithmetic and copies ran while one was open for 0% of the time, Pallas kernels for 5%

profile of v5, /device:TPU:0, one launch (start us, length us, event | category | flops | bytes accessed | tf_op | source)
XLA Modules:
  0.0 14.7 jit_solution(15839188479400131601)
XLA Ops:
  0.0 1.2 %encode.1 = f32[16,2,128]{2,1,0:T(2,128)S(1)} custom-call(s32[2,16,8,128]{3,2,1,0:T(8,128)} %bitcast.13, s32[1,2]{1,0:T(1,128)} %bitcast.17, f32[2,16]{1,0:T(2,128)} %bitcast.15, f32[2,16]{1,0:T(2,128)} %bitcast.16, f32[3,2,16]{2,1,0:T(2,128)} %bitcast.14), custom_call_target="tpu_custom_call" | custom-call | flops 1000000 | bytes 1000000 | tf_op jit(solution)/shard_map/encode/pallas_call | solution.py:212
  1.2 11.3 %all_to_all.5.refs_0_ = f32[16,2,128]{2,1,0:T(2,128)S(1)} all-to-all(f32[16,2,128]{2,1,0:T(2,128)S(1)} %encode.1), channel_id=1, replica_groups={{31,30,29,28,19,18,17,16,15,14,5,4,3,2,1,0},{23,22,21,20,27,26,25,24,7,..., dimensions={0} | all-to-all | bytes 32768 | tf_op jit(solution)/shard_map/all_to_all | solution.py:237
  12.6 0.4 %collective-permute-start = (f32[1,128]{1,0:T(1,128)S(1)}, f32[1,128]{1,0:T(1,128)S(1)}, u32[]{:S(2)}, u32[]{:S(2)}) collective-permute-start(f32[1,128]{1,0:T(1,128)S(1)} %bitcast.11), channel_id=1, source_target_pairs={{0,8},{8,0},{16,24},{24,16},{1,9},{9,1},{17,25},{25,17},{2,10},{10... | collective-permute-start | bytes 1544 | tf_op jit(solution)/shard_map/ppermute | solution.py:239
  12.9 0.8 %assemble.1.refs_2_ = f32[9,128,128]{2,1,0:T(8,128)S(1)} custom-call(f32[16,2,128]{2,1,0:T(2,128)S(1)} %all_to_all.5.refs_0_), custom_call_target="tpu_custom_call" | custom-call | flops 150994944 | bytes 1000000 | tf_op jit(solution)/shard_map/assemble/pallas_call | solution.py:241
  13.7 0.1 collective-permute-done.refs_1_
  13.8 0.9 %scale.1 = f32[9,128,128]{2,1,0:T(8,128)} custom-call(f32[1,128]{1,0:T(1,128)S(1)} %bitcast.12, f32[1,128]{1,0:T(1,128)S(1)} %collective-permute-done.refs_1_, f32[9,128,128]{2,1,0:T(8,128)S(1)} %assemble.1.refs_2_), custom_call_target="tpu_custom_call" | custom-call | flops 1000000 | bytes 1000000 | tf_op jit(solution)/shard_map/scale/pallas_call | solution.py:250
  (1 shorter events, 0.0 us)
Async XLA Ops:
  12.6 1.2 %collective-permute-start = (f32[1,128]{1,0:T(1,128)S(1)}, f32[1,128]{1,0:T(1,128)S(1)}, u32[]{:S(2)}, u32[]{:S(2)}) collective-permute-start(f32[1,128]{1,0:T(1,128)S(1)} %bitcast.11), channel_id=1, source_target_pairs={{0,8},{8,0},{16,24},{24,16},{1,9},{9,1},{17,25},{25,17},{2,10},{10... | collective-permute-start | bytes 1544 | tf_op jit(solution)/shard_map/ppermute | solution.py:239

commit v6 on v5

--- a/solution.py
+++ b/solution.py
@@ -9,7 +9,7 @@
 
 AXES = ("gx", "gy", "gz")
 VMEM_LIMIT = 16 * 2**20
-CUTS = (0, 3, 6, 9)
+CUTS = (0, 2, 5, 9)
 FIELDS = 8
 DIAGONAL = 2.0 / 9.0
 

time: 14.9 us -> 14.9 us (level)
  no operation moved by 1% of the time
where the time goes in v6:
time: 14.9 us; the launch traced here: 14.7 us
  blocking collectives  11.3 us (76%)
  Pallas kernels  2.91 us (20%)
  starting transfers between devices  0.37 us (2%)
    all_to_all x1, blocking collectives, on_device(): lax.all_to_all(payload, AXES, 0, 0, axis_index_groups=groups, tiled=True)  11.3 us
    pallas_call x1, Pallas kernels, on_device(): call(lambda *refs: encode_kernel(targets, *refs), 'encode', jax.ShapeDtyp...  1.21 us
    pallas_call x1, Pallas kernels, on_device(): call(lambda *refs: scale_kernel(entries, *refs), 'scale', block_shape, [v...  0.92 us
    pallas_call x1, Pallas kernels, on_device(): call(lambda *refs: assemble_kernel(depth, cap, place, *refs), 'assemble',...  0.78 us
    ppermute x1, starting transfers between devices, on_device(): swapped = lax.ppermute(parts, 'gx', [(i, i ^ 1) for i in range(n_gx)])  0.37 us
  transfers between devices with their start and end apart: 1, of which 1 were waited for; matrix products, arithmetic and copies ran while one was open for 0% of the time, Pallas kernels for 5%

profile of v6, /device:TPU:0, one launch (start us, length us, event | category | flops | bytes accessed | tf_op | source)
XLA Modules:
  0.0 14.7 jit_solution(16336890666391181036)
XLA Ops:
  0.0 1.2 %encode.1 = f32[16,2,128]{2,1,0:T(2,128)S(1)} custom-call(s32[2,16,8,128]{3,2,1,0:T(8,128)} %bitcast.13, s32[1,2]{1,0:T(1,128)} %bitcast.17, f32[2,16]{1,0:T(2,128)} %bitcast.15, f32[2,16]{1,0:T(2,128)} %bitcast.16, f32[3,2,16]{2,1,0:T(2,128)} %bitcast.14), custom_call_target="tpu_custom_call" | custom-call | flops 1000000 | bytes 1000000 | tf_op jit(solution)/shard_map/encode/pallas_call | solution.py:212
  1.2 11.3 %all_to_all.5.refs_0_ = f32[16,2,128]{2,1,0:T(2,128)S(1)} all-to-all(f32[16,2,128]{2,1,0:T(2,128)S(1)} %encode.1), channel_id=1, replica_groups={{31,30,29,28,19,18,17,16,15,14,5,4,3,2,1,0},{23,22,21,20,27,26,25,24,7,..., dimensions={0} | all-to-all | bytes 32768 | tf_op jit(solution)/shard_map/all_to_all | solution.py:237
  12.6 0.4 %collective-permute-start = (f32[1,128]{1,0:T(1,128)S(1)}, f32[1,128]{1,0:T(1,128)S(1)}, u32[]{:S(2)}, u32[]{:S(2)}) collective-permute-start(f32[1,128]{1,0:T(1,128)S(1)} %bitcast.11), channel_id=1, source_target_pairs={{0,8},{8,0},{16,24},{24,16},{1,9},{9,1},{17,25},{25,17},{2,10},{10... | collective-permute-start | bytes 1544 | tf_op jit(solution)/shard_map/ppermute | solution.py:239
  12.9 0.8 %assemble.1.refs_2_ = f32[9,128,128]{2,1,0:T(8,128)S(1)} custom-call(f32[16,2,128]{2,1,0:T(2,128)S(1)} %all_to_all.5.refs_0_), custom_call_target="tpu_custom_call" | custom-call | flops 150994944 | bytes 1000000 | tf_op jit(solution)/shard_map/assemble/pallas_call | solution.py:241
  13.7 0.1 collective-permute-done.refs_1_
  13.8 0.9 %scale.1 = f32[9,128,128]{2,1,0:T(8,128)} custom-call(f32[1,128]{1,0:T(1,128)S(1)} %bitcast.12, f32[1,128]{1,0:T(1,128)S(1)} %collective-permute-done.refs_1_, f32[9,128,128]{2,1,0:T(8,128)S(1)} %assemble.1.refs_2_), custom_call_target="tpu_custom_call" | custom-call | flops 1000000 | bytes 1000000 | tf_op jit(solution)/shard_map/scale/pallas_call | solution.py:250
  (1 shorter events, 0.0 us)
Async XLA Ops:
  12.6 1.2 %collective-permute-start = (f32[1,128]{1,0:T(1,128)S(1)}, f32[1,128]{1,0:T(1,128)S(1)}, u32[]{:S(2)}, u32[]{:S(2)}) collective-permute-start(f32[1,128]{1,0:T(1,128)S(1)} %bitcast.11), channel_id=1, source_target_pairs={{0,8},{8,0},{16,24},{24,16},{1,9},{9,1},{17,25},{25,17},{2,10},{10... | collective-permute-start | bytes 1544 | tf_op jit(solution)/shard_map/ppermute | solution.py:239

commit v7 on v6

--- a/solution.py
+++ b/solution.py
@@ -54,6 +54,12 @@
     spread = (line == lax.broadcasted_iota(jnp.int32, (cap, lanes), 1) // corners).astype(jnp.float32)
     for copy in small:
         copy.wait()
+    large.wait()
+    live = [lane // corners < live_ref[:, t : t + 1] for t in range(tiles)]
+    partial = jnp.zeros((1, lanes), jnp.float32)
+    node_ids = []
+    onehot = inc_ref[...].reshape(tiles * lanes, width)
+    found = last_contraction(reader, onehot.astype(jnp.float32).astype(jnp.bfloat16))
     lame, shear = params_ref[0], params_ref[1]
     lengths = [params_ref[2 + k] for k in range(3)]
     inverse = [2.0 / length for length in lengths]
@@ -72,12 +78,6 @@
         fields = jnp.concatenate([fields, jnp.zeros((FIELDS, lanes - cap), jnp.float32)], axis=1)
         fields = pltpu.roll(fields, 0, axis=1, stride=cap, stride_axis=0)
         field_rows.append(jnp.sum(fields, axis=0, keepdims=True))
-    live = [lane // corners < live_ref[:, t : t + 1] for t in range(tiles)]
-    large.wait()
-    partial = jnp.zeros((1, lanes), jnp.float32)
-    node_ids = []
-    onehot = inc_ref[...].reshape(tiles * lanes, width)
-    found = last_contraction(reader, onehot.astype(jnp.float32).astype(jnp.bfloat16))
     for t in range(tiles):
         position = found[0:1, t * lanes : (t + 1) * lanes]
         here = (found[1:2, t * lanes : (t + 1) * lanes] > 0.5) & live[t]

time: 14.9 us -> 14.9 us (level)
  no operation moved by 1% of the time
where the time goes in v7:
time: 14.9 us; the launch traced here: 14.6 us
  blocking collectives  11.3 us (76%)
  Pallas kernels  2.86 us (19%)
  starting transfers between devices  0.37 us (2%)
    all_to_all x1, blocking collectives, on_device(): lax.all_to_all(payload, AXES, 0, 0, axis_index_groups=groups, tiled=True)  11.3 us
    pallas_call x1, Pallas kernels, on_device(): call(lambda *refs: encode_kernel(targets, *refs), 'encode', jax.ShapeDtyp...  1.15 us
    pallas_call x1, Pallas kernels, on_device(): call(lambda *refs: scale_kernel(entries, *refs), 'scale', block_shape, [v...  0.92 us
    pallas_call x1, Pallas kernels, on_device(): call(lambda *refs: assemble_kernel(depth, cap, place, *refs), 'assemble',...  0.78 us
    ppermute x1, starting transfers between devices, on_device(): swapped = lax.ppermute(parts, 'gx', [(i, i ^ 1) for i in range(n_gx)])  0.37 us
  transfers between devices with their start and end apart: 1, of which 1 were waited for; matrix products, arithmetic and copies ran while one was open for 0% of the time, Pallas kernels for 5%

profile of v7, /device:TPU:0, one launch (start us, length us, event | category | flops | bytes accessed | tf_op | source)
XLA Modules:
  0.0 14.6 jit_solution(8101653766103332112)
XLA Ops:
  0.0 1.2 %encode.1 = f32[16,2,128]{2,1,0:T(2,128)S(1)} custom-call(s32[2,16,8,128]{3,2,1,0:T(8,128)} %bitcast.13, s32[1,2]{1,0:T(1,128)} %bitcast.17, f32[2,16]{1,0:T(2,128)} %bitcast.15, f32[2,16]{1,0:T(2,128)} %bitcast.16, f32[3,2,16]{2,1,0:T(2,128)} %bitcast.14), custom_call_target="tpu_custom_call" | custom-call | flops 1000000 | bytes 1000000 | tf_op jit(solution)/shard_map/encode/pallas_call | solution.py:212
  1.2 11.3 %all_to_all.5.refs_0_ = f32[16,2,128]{2,1,0:T(2,128)S(1)} all-to-all(f32[16,2,128]{2,1,0:T(2,128)S(1)} %encode.1), channel_id=1, replica_groups={{31,30,29,28,19,18,17,16,15,14,5,4,3,2,1,0},{23,22,21,20,27,26,25,24,7,..., dimensions={0} | all-to-all | bytes 32768 | tf_op jit(solution)/shard_map/all_to_all | solution.py:237
  12.5 0.4 %collective-permute-start = (f32[1,128]{1,0:T(1,128)S(1)}, f32[1,128]{1,0:T(1,128)S(1)}, u32[]{:S(2)}, u32[]{:S(2)}) collective-permute-start(f32[1,128]{1,0:T(1,128)S(1)} %bitcast.11), channel_id=1, source_target_pairs={{0,8},{8,0},{16,24},{24,16},{1,9},{9,1},{17,25},{25,17},{2,10},{10... | collective-permute-start | bytes 1544 | tf_op jit(solution)/shard_map/ppermute | solution.py:239
  12.9 0.8 %assemble.1.refs_2_ = f32[9,128,128]{2,1,0:T(8,128)S(1)} custom-call(f32[16,2,128]{2,1,0:T(2,128)S(1)} %all_to_all.5.refs_0_), custom_call_target="tpu_custom_call" | custom-call | flops 150994944 | bytes 1000000 | tf_op jit(solution)/shard_map/assemble/pallas_call | solution.py:241
  13.7 0.1 collective-permute-done.refs_1_
  13.7 0.9 %scale.1 = f32[9,128,128]{2,1,0:T(8,128)} custom-call(f32[1,128]{1,0:T(1,128)S(1)} %bitcast.12, f32[1,128]{1,0:T(1,128)S(1)} %collective-permute-done.refs_1_, f32[9,128,128]{2,1,0:T(8,128)S(1)} %assemble.1.refs_2_), custom_call_target="tpu_custom_call" | custom-call | flops 1000000 | bytes 1000000 | tf_op jit(solution)/shard_map/scale/pallas_call | solution.py:250
  (1 shorter events, 0.0 us)
Async XLA Ops:
  12.5 1.2 %collective-permute-start = (f32[1,128]{1,0:T(1,128)S(1)}, f32[1,128]{1,0:T(1,128)S(1)}, u32[]{:S(2)}, u32[]{:S(2)}) collective-permute-start(f32[1,128]{1,0:T(1,128)S(1)} %bitcast.11), channel_id=1, source_target_pairs={{0,8},{8,0},{16,24},{24,16},{1,9},{9,1},{17,25},{25,17},{2,10},{10... | collective-permute-start | bytes 1544 | tf_op jit(solution)/shard_map/ppermute | solution.py:239
